TPU v7x, 32 devices: a whole 2x2x4 slice. The times are simulated.
32 devices in a mesh: sector: 8 (over y, x, core), block: 4 (over z).
Axes of the slice: x: 2, y: 2, z: 4, core: 2. Of those that a mesh axis runs over, the one named last changes fastest.
Arguments:
- source: float32 [125, 2, 128, 512], P(None, None, 'sector', 'block'), may hold values from -6 to 6
- jacobian: float32 [2, 128, 512], P(None, 'sector', 'block'), may hold values from 0.5 to 2
- stiff_fine: float32 [125, 125], replicated, may hold values from -1 to 2, as said below
- stiff_coarse: float32 [27, 27], replicated, may hold values from -1 to 2, as said below
- restrict_fine: float32 [27, 125], replicated, may hold values from -0.5 to 0.5
- restrict_coarse: float32 [8, 27], replicated, may hold values from -1.25 to 1.25
- mortar_proj: float32 [2, 5, 5], replicated, may hold values from -2.5 to 2.5
- rotor_trace: float32 [4, 25, 128, 512], P(None, None, 'sector', 'block'), may hold values from -6 to 6
- stator_trace: float32 [4, 25, 128, 512], P(None, None, 'sector', 'block'), may hold values from -6 to 6
- offsets: int32 [4], P('block'), may hold values from 0 to 127
Outputs:
- stator_flux: float32 [4, 25, 128, 512], P(None, None, 'sector', 'block')
- rotor_flux: float32 [4, 25, 128, 512], P(None, None, 'sector', 'block')
- fine_pressure: float32 [125, 2, 128, 512], P(None, None, 'sector', 'block')
- coarse_pressure: float32 [27, 2, 128, 512], P(None, None, 'sector', 'block')
- coarsest_residual: float32 [8, 2, 128, 512], P(None, None, 'sector', 'block')
Inputs may be any that keep to these rules, and one draw needn't show every extreme that they name: `stiff_fine`: symmetric, positive diagonal. `stiff_coarse`: symmetric, positive diagonal.
All inputs are finite; a program needn't handle non-finite values.
Results may differ from a plain program's by a relative error of at most 0.00016.
Values sent between devices are 32-bit elements; how exact they have to be, the bound alone decides.
No kernel may reach another device: no remote copies, remote signals or barrier semaphores. Data moves between devices by JAX's collectives and lax.ppermute only.
A program may use at most 128 MiB of HBM per device.

v0:
```python
import jax
import jax.numpy as jnp
from jax import lax
from jax.experimental import pallas as pl
from jax.experimental.pallas import tpu as pltpu
from jax.sharding import PartitionSpec as P


F32 = jnp.float32
BF16 = jnp.bfloat16
DAMPING = 0.6
PENALTY = 0.5
LANES = 128
NF = 5
NC = 3
LAST = 8
STEP = 4
FACE_UNROLL = 5
HALO_UNROLL = 32
GROUP = {NF: 4, NC: 16}
GROUP_UNROLL = {NF: 4, NC: 1}
VMEM_BYTES = 12 * 1024 * 1024


def up(value, unit):
    return (value + unit - 1) // unit * unit


def any_spec():
    return pl.BlockSpec(memory_space=pl.ANY)


def hbm_spec():
    return pl.BlockSpec(memory_space=pltpu.HBM)


def in_hbm(*arrays):
    return tuple(pltpu.with_memory_space_constraint(x, pltpu.HBM) for x in arrays)


def params(**extra):
    return pltpu.CompilerParams(vmem_limit_bytes=VMEM_BYTES, **extra)


def cost(flops, data):
    return pl.CostEstimate(flops=flops, bytes_accessed=data, transcendentals=0)


def parts_of(x):
    high = x.astype(BF16)
    low = (x - high.astype(F32)).astype(BF16)
    return high, low


def stacked(matrix):
    high, low = parts_of(matrix)
    top = jnp.concatenate([high, high], axis=1)
    bottom = jnp.concatenate([low, jnp.zeros_like(low)], axis=1)
    return jnp.concatenate([top, bottom], axis=0)


def times(weights, x):
    rows = weights.shape[0] // 2
    high, low = parts_of(x)
    both = jnp.dot(weights, jnp.concatenate([high, low], axis=0), preferred_element_type=F32)
    return both[:rows] + both[rows:]


def lane_ids(rows):
    return lax.broadcasted_iota(jnp.int32, (rows, LANES), 1)


def node_rows(shape, axis):
    return lax.broadcasted_iota(jnp.int32, shape, axis)


def digit(index, unit, most):
    found = jnp.zeros_like(index)
    for k in range(1, most + 1):
        found += jnp.where(index >= k * unit, 1, 0)
    return found


def half_faces(n, height):
    row = node_rows((height, LANES), 0)
    a = digit(row, n * n, n)
    b = digit(row - n * n * a, n, n - 1)
    on_a = jnp.where((a == 0) | (a == n - 1), PENALTY, 0.0)
    on_b = jnp.where((b == 0) | (b == n - 1), PENALTY, 0.0)
    return jnp.where(row < n**3, on_a + on_b, 0.0)


def add_halo(n, e_total, span, source_of, r_ref, c1, c2, z1, z2):
    nn = n * n
    odd = lax.rem(lax.axis_index("sector"), 2) == 1
    block = lax.axis_index("block")
    z_odd = lax.rem(block, 2) == 1
    lowest = block == 0
    highest = block == lax.axis_size("block") - 1
    lanes = lane_ids(8)

    def slab(e, carry):
        r_ref[e] = source_of(e)
        for a in range(n):
            first, second = z1[a], z2[a]
            below = jnp.where(z_odd, first, second)
            above = jnp.where(z_odd, second, first)
            below = pltpu.roll(below, lax.rem(LANES - e, LANES), 1)
            above = pltpu.roll(above, LANES - 1 - e, 1)
            below = jnp.where((lanes == 0) & jnp.logical_not(lowest), PENALTY * below, 0.0)
            above = jnp.where((lanes == LANES - 1) & jnp.logical_not(highest), PENALTY * above, 0.0)
            r_ref[e, pl.ds(a * nn, n), :] += below[:n]
            r_ref[e, pl.ds(a * nn + nn - n, n), :] += above[:n]
        return carry

    lax.fori_loop(0, e_total, slab, 0, unroll=HALO_UNROLL)
    for layer in range(e_total // span):
        first, second = c1[layer], c2[layer]
        r_ref[layer * span, pl.ds(0, nn), :] += PENALTY * jnp.where(odd, first, second)
        r_ref[layer * span + span - 1, pl.ds((n - 1) * nn, nn), :] += PENALTY * jnp.where(odd, second, first)


def correct(n, e_total, span, r_ref, u_ref, u_of, c1, c2, z1, z2):
    nn = n * n
    lanes = lane_ids(8)

    def slab(e, carry):
        lows, highs = carry
        u_ref[e] = u_of(e, r_ref[e])
        new_lows, new_highs = [], []
        for a in range(n):
            low = u_ref[e, pl.ds(a * nn, 8), :]
            high = u_ref[e, pl.ds(a * nn + nn - n, 8), :]
            here = lanes == e
            new_lows.append(jnp.where(here, pltpu.roll(low, e, 1), lows[a]))
            new_highs.append(jnp.where(here, pltpu.roll(high, e + 1, 1), highs[a]))
        return tuple(new_lows), tuple(new_highs)

    blank = tuple(jnp.zeros((8, LANES), F32) for _ in range(n))
    lows, highs = lax.fori_loop(0, e_total, slab, (blank, blank), unroll=HALO_UNROLL)
    odd = lax.rem(lax.axis_index("sector"), 2) == 1
    z_odd = lax.rem(lax.axis_index("block"), 2) == 1
    for a in range(n):
        z1[a] = jnp.where(z_odd, lows[a], highs[a])
        z2[a] = jnp.where(z_odd, highs[a], lows[a])
    for layer in range(e_total // span):
        low = u_ref[layer * span, pl.ds(0, nn), :]
        high = u_ref[layer * span + span - 1, pl.ds((n - 1) * nn, nn), :]
        c1[layer] = jnp.where(odd, low, high)
        c2[layer] = jnp.where(odd, high, low)


def subtract_operator(n, e_total, span, r_ref, u_ref, weights, jac_ref, count_ref):
    nn = n * n
    group = GROUP[n]
    lanes = lane_ids(8)

    def some(i, carry):
        first = i * group
        wide = jnp.concatenate([u_ref[first + j] for j in range(group)], axis=1)
        product = times(weights[...], wide)
        for j in range(group):
            e = first + j
            own = product[:, j * LANES : (j + 1) * LANES]
            r_ref[e] = r_ref[e] - jac_ref[pl.ds(e, 1), :] * own - count_ref[...] * u_ref[e]
            s = lax.rem(e, span)
            before = jnp.where(s > 0, PENALTY, 0.0)
            after = jnp.where(s < span - 1, PENALTY, 0.0)
            previous = u_ref[jnp.maximum(e - 1, 0), pl.ds((n - 1) * nn, nn), :]
            following = u_ref[jnp.minimum(e + 1, e_total - 1), pl.ds(0, nn), :]
            r_ref[e, pl.ds(0, nn), :] += before * previous
            r_ref[e, pl.ds((n - 1) * nn, nn), :] += after * following
            for a in range(n):
                low = u_ref[e, pl.ds(a * nn, 8), :]
                high = u_ref[e, pl.ds(a * nn + nn - n, 8), :]
                from_below = jnp.where(lanes > 0, PENALTY * pltpu.roll(high, 1, 1), 0.0)
                from_above = jnp.where(lanes < LANES - 1, PENALTY * pltpu.roll(low, LANES - 1, 1), 0.0)
                r_ref[e, pl.ds(a * nn, n), :] += from_below[:n]
                r_ref[e, pl.ds(a * nn + nn - n, n), :] += from_above[:n]
        return carry

    lax.fori_loop(0, e_total // group, some, 0, unroll=GROUP_UNROLL[n])


def face_shapes(n, layers):
    circ = jax.ShapeDtypeStruct((layers, n * n, LANES), F32)
    axial = jax.ShapeDtypeStruct((n, 8, LANES), F32)
    return [circ, circ, axial, axial]


def prepare(rotor, stator, mortar, stiff_fine, stiff_coarse, restrict_fine, restrict_coarse):
    rows, span = rotor.shape[0], rotor.shape[1]
    tall, wide = up(rows, 8), up(rows, 16)
    big, small = up(NF**3, 16), up(NC**3, 16)
    smalls = (mortar, stiff_fine, stiff_coarse, restrict_fine, restrict_coarse)

    def body(
        rotor_ref, stator_ref, mortar_in, kf_in, kc_in, rf_in, rc_in,
        rotor_out, stator_out, proj_out, back_out, wf_out, wc_out, rfs_out, rcs_out, df_out, dc_out,
        mortar_ref, kf_ref, kc_ref, rf_ref, rc_ref, pad_ref, sem, small_sem,
    ):
        copies = []
        for f in range(span):
            for source, target in ((rotor_ref, rotor_out), (stator_ref, stator_out)):
                if tall > rows:
                    target[f, pl.ds(rows, tall - rows), :] = jnp.zeros((tall - rows, LANES), F32)
                copies.append(pltpu.make_async_copy(source.at[:, f, :], target.at[f, pl.ds(0, rows), :], sem))
        little = [
            pltpu.make_async_copy(source, target, small_sem)
            for source, target in (
                (mortar_in, mortar_ref), (kf_in, kf_ref), (kc_in, kc_ref), (rf_in, rf_ref), (rc_in, rc_ref)
            )
        ]
        for c in little + copies:
            c.start()
        row, col = node_rows((tall, LANES), 0), node_rows((tall, LANES), 1)
        comp_r, comp_c = digit(row, NF * NF, 4), digit(col, NF * NF, 5)
        rest_r, rest_c = row - NF * NF * comp_r, col - NF * NF * comp_c
        a_r, a_c = digit(rest_r, NF, NF - 1), digit(rest_c, NF, NF - 1)
        same = (comp_r == comp_c) & (rest_r - NF * a_r == rest_c - NF * a_c) & (row < rows) & (col < rows)
        ahead = jnp.where(same, a_r * NF + a_c, -1)
        flipped = jnp.where(same, a_c * NF + a_r, -1)
        for c in little:
            c.wait()
        for found, out in ((ahead, proj_out), (flipped, back_out)):
            pair = []
            for which in range(2):
                total = jnp.zeros((tall, LANES), F32)
                matrix = mortar_ref[:, which, :]
                for i in range(NF):
                    for j in range(NF):
                        total = jnp.where(found == i * NF + j, matrix[i : i + 1, j : j + 1], total)
                pair.append(total[:, :wide])
            highs, lows = zip(*[parts_of(m) for m in pair])
            out[...] = jnp.concatenate(
                [
                    jnp.concatenate([jnp.concatenate([h, h], axis=1) for h in highs], axis=0),
                    jnp.concatenate([jnp.concatenate([l, jnp.zeros_like(l)], axis=1) for l in lows], axis=0),
                ],
                axis=0,
            )

        def padded(ref, height, width):
            pad_ref[...] = jnp.zeros_like(pad_ref)
            pad_ref[pl.ds(0, ref.shape[0]), pl.ds(0, ref.shape[1])] = ref[...]
            return pad_ref[pl.ds(0, height), :][:, :width]

        for ref, out, diag_out, size in ((kf_ref, wf_out, df_out, big), (kc_ref, wc_out, dc_out, small)):
            matrix = padded(ref, size, size)
            out[...] = stacked(matrix)
            row = lax.broadcasted_iota(jnp.int32, (size, size), 0)
            col = lax.broadcasted_iota(jnp.int32, (size, size), 1)
            diag = jnp.sum(jnp.where(row == col, matrix, 0.0), axis=1, keepdims=True)
            diag = jnp.where(row[:, :1] < ref.shape[0], diag, 1.0)
            diag_out[...] = jnp.broadcast_to(diag, (size, LANES))
        rfs_out[...] = stacked(padded(rf_ref, small, big))
        rcs_out[...] = stacked(padded(rc_ref, 16, small))
        for c in copies:
            c.wait()

    return pl.pallas_call(
        body,
        out_shape=[
            jax.ShapeDtypeStruct((span, tall, LANES), F32),
            jax.ShapeDtypeStruct((span, tall, LANES), F32),
            jax.ShapeDtypeStruct((4 * tall, 2 * wide), BF16),
            jax.ShapeDtypeStruct((4 * tall, 2 * wide), BF16),
            jax.ShapeDtypeStruct((2 * big, 2 * big), BF16),
            jax.ShapeDtypeStruct((2 * small, 2 * small), BF16),
            jax.ShapeDtypeStruct((2 * small, 2 * big), BF16),
            jax.ShapeDtypeStruct((32, 2 * small), BF16),
            jax.ShapeDtypeStruct((big, LANES), F32),
            jax.ShapeDtypeStruct((small, LANES), F32),
        ],
        in_specs=[hbm_spec()] * 7,
        scratch_shapes=[pltpu.VMEM(m.shape, F32) for m in smalls]
        + [pltpu.VMEM((big, LANES), F32), pltpu.SemaphoreType.DMA, pltpu.SemaphoreType.DMA],
        compiler_params=params(),
        name="prepare",
    )(*in_hbm(rotor, stator, *smalls))


def apply_faces(matrix_ref, slab_of, count, tall, wide, y0, y1, unroll=1):
    group = 4
    fill = jnp.zeros((wide - tall, group * LANES), F32)

    def some(i, carry):
        first = group * i
        x = jnp.concatenate([slab_of(jnp.minimum(first + j, count - 1)) for j in range(group)], axis=1)
        if wide > tall:
            x = jnp.concatenate([x, fill], axis=0)
        high, low = parts_of(x)
        y = jnp.dot(matrix_ref[...], jnp.concatenate([high, low], axis=0), preferred_element_type=F32)
        a = y[:tall] + y[2 * tall : 3 * tall]
        b = y[tall : 2 * tall] + y[3 * tall :]
        for j in range(group):
            y0[first + j] = a[:, j * LANES : (j + 1) * LANES]
            y1[first + j] = b[:, j * LANES : (j + 1) * LANES]
        return carry

    lax.fori_loop(0, up(count, group) // group, some, 0, unroll=unroll)


def own_part(rotor, near1, near2, proj, jac, diag):
    span, tall = rotor.shape[0], rotor.shape[1]
    wide = proj.shape[1] // 2
    e_total, height = jac.shape[0], diag.shape[0]

    def body(r_in, near1_ref, near2_ref, proj_ref, jac_ref, diag_ref, kept, w_ref, y0, y1):
        odd = lax.rem(lax.axis_index("sector"), 2) == 1
        before = jnp.where(odd, near1_ref[0], near2_ref[0])
        after = jnp.where(odd, near2_ref[0], near1_ref[0])

        def rotor_slab(f):
            inside = r_in[jnp.clip(f - 1, 0, span - 1)]
            return jnp.where(f == 0, before, jnp.where(f == span + 1, after, inside))

        apply_faces(proj_ref, rotor_slab, span + 2, tall, wide, y0, y1)

        def face(g, carry):
            kept[g] = y0[g + 1] + y1[g]
            return carry

        lax.fori_loop(0, span + 1, face, 0)
        count = half_faces(NF, height)

        def weight(e, carry):
            w_ref[e] = DAMPING / (jac_ref[pl.ds(e, 1), :] * diag_ref[...] + count)
            return carry

        lax.fori_loop(0, e_total, weight, 0)

    return pl.pallas_call(
        body,
        out_shape=[
            jax.ShapeDtypeStruct((span + 1, tall, LANES), F32),
            jax.ShapeDtypeStruct((e_total, height, LANES), F32),
        ],
        scratch_shapes=[pltpu.VMEM((up(span + 2, 4), tall, LANES), F32)] * 2,
        compiler_params=params(),
        cost_estimate=cost(2 * 10**9, 10 * 10**6),
        name="own_part",
    )(rotor, near1, near2, proj, jac, diag)


def join(far, near, near_s, far_s):
    few, many = far.shape[0], near.shape[0]
    window = jax.ShapeDtypeStruct((few + many,) + far.shape[1:], F32)

    def body(far_ref, near_ref, near_s_ref, far_s_ref, rotor_out, stator_out):
        def copy(source, out, first):
            def one(f, carry):
                out[first + f] = source[f]
                return carry

            lax.fori_loop(0, source.shape[0], one, 0)

        copy(far_ref, rotor_out, 0)
        copy(near_ref, rotor_out, few)
        copy(near_s_ref, stator_out, 0)
        copy(far_s_ref, stator_out, many)

    return pl.pallas_call(body, out_shape=[window, window], compiler_params=params(), name="join")(
        far, near, near_s, far_s
    )


def first_sweep(shift, rotor_win, stator_win, stator, kept, proj, back, source, w, jac, weights, layers):
    span, tall = stator.shape[0], stator.shape[1]
    wide = back.shape[1] // 2
    rows = 4 * NF * NF
    e_total = jac.shape[0]
    n, nn = NF, NF * NF
    nodes = n**3
    height = weights.shape[0] // 2

    def body(
        shift_ref, rw_ref, sw_ref, s_in, kept_ref, proj_ref, back_ref, source_ref, w_ref, jac_ref, w_mat,
        sflux_out, rflux_out, r_ref, u_ref, c1, c2, z1, z2,
        y0, y1, x0, x1, sflux, rflux, count_ref, in_sem, out_sem,
    ):
        loads = [
            pltpu.make_async_copy(source_ref.at[:, e, :], r_ref.at[e, pl.ds(0, nodes), :], in_sem)
            for e in range(e_total)
        ]
        for c in loads:
            c.start()
        inner = shift_ref[0]
        first_rotor = STEP - 1 - inner
        count_ref[...] = half_faces(n, height)
        apply_faces(proj_ref, lambda f: rw_ref[first_rotor + f], span + 1, tall, wide, x0, x1, unroll=FACE_UNROLL)
        apply_faces(
            back_ref, lambda f: sw_ref[inner + f] - kept_ref[f], span + 1, tall, wide, y0, y1, unroll=FACE_UNROLL
        )
        stores = []
        for s in range(span):
            sflux[s] = s_in[s] - (x0[s + 1] + x1[s])
            rflux[s] = y0[s] + y1[s + 1]
            for buffer, out in ((sflux, sflux_out), (rflux, rflux_out)):
                c = pltpu.make_async_copy(buffer.at[s, pl.ds(0, rows), :], out.at[:, s, :], out_sem)
                c.start()
                stores.append(c)
        for c in loads:
            c.wait()
        for s in range(span):
            if height > nodes:
                for layer in range(layers):
                    r_ref[layer * span + s, pl.ds(nodes, height - nodes), :] = jnp.zeros((height - nodes, LANES), F32)
            inflow = sflux[s, pl.ds(0, nn), :] + sflux[s, pl.ds(3 * nn, nn), :]
            outflow = rflux[s, pl.ds(0, nn), :] + rflux[s, pl.ds(3 * nn, nn), :]
            r_ref[span + s, pl.ds(0, nn, stride=n), :] += inflow
            r_ref[s, pl.ds(n - 1, nn, stride=n), :] += -outflow
        correct(n, e_total, span, r_ref, u_ref, lambda e, r: r * w_ref[e], c1, c2, z1, z2)
        subtract_operator(n, e_total, span, r_ref, u_ref, w_mat, jac_ref, count_ref)
        for c in stores:
            c.wait()

    whole = pl.BlockSpec()
    field = jax.ShapeDtypeStruct((e_total, height, LANES), F32)
    trace = jax.ShapeDtypeStruct((rows, span, LANES), F32)
    slabs = pltpu.VMEM((up(span + 1, 4), tall, LANES), F32)
    return pl.pallas_call(
        body,
        out_shape=[trace, trace, field, field] + face_shapes(n, layers),
        in_specs=[pl.BlockSpec(memory_space=pltpu.SMEM)] + [whole] * 6 + [hbm_spec()] + [whole] * 3,
        out_specs=[hbm_spec()] * 2 + [whole] * 6,
        scratch_shapes=[slabs] * 4
        + [
            pltpu.VMEM((span, tall, LANES), F32),
            pltpu.VMEM((span, tall, LANES), F32),
            pltpu.VMEM((height, LANES), F32),
            pltpu.SemaphoreType.DMA,
            pltpu.SemaphoreType.DMA,
        ],
        compiler_params=params(),
        cost_estimate=cost(2 * 10**9, 20 * 10**6),
        name="first_sweep",
    )(shift, rotor_win, stator_win, stator, kept, proj, back, *in_hbm(source), w, jac, weights)


def sweep(n, r, p, w, jac, weights, faces, layers, last):
    e_total, height = r.shape[0], r.shape[1]
    span = e_total // layers
    nodes = n**3

    def body(r_in, p_in, w_in, jac_ref, w_mat, h1, h2, g1, g2, p_out, r_ref, c1, c2, z1, z2, u_ref, p_keep, count_ref, sem):
        count_ref[...] = half_faces(n, height)
        p_ref = p_keep if last else p_out
        add_halo(n, e_total, span, lambda e: r_in[e], r_ref, h1, h2, g1, g2)

        def u_of(e, r_here):
            u = r_here * w_in[e]
            p_ref[e] = p_in[e] + u
            return u

        correct(n, e_total, span, r_ref, u_ref, u_of, c1, c2, z1, z2)
        stores = []
        if last:
            for e in range(e_total):
                c = pltpu.make_async_copy(p_ref.at[e, pl.ds(0, nodes), :], p_out.at[:, e, :], sem)
                c.start()
                stores.append(c)
        subtract_operator(n, e_total, span, r_ref, u_ref, w_mat, jac_ref, count_ref)
        for c in stores:
            c.wait()

    whole = pl.BlockSpec()
    field = jax.ShapeDtypeStruct((e_total, height, LANES), F32)
    kept = jax.ShapeDtypeStruct((nodes, e_total, LANES), F32) if last else field
    return pl.pallas_call(
        body,
        out_shape=[kept, field] + face_shapes(n, layers),
        out_specs=[any_spec() if last else whole] + [whole] * 5,
        scratch_shapes=[
            pltpu.VMEM((e_total, height, LANES), F32),
            pltpu.VMEM((e_total, height, LANES) if last else (1, 8, LANES), F32),
            pltpu.VMEM((height, LANES), F32),
            pltpu.SemaphoreType.DMA,
        ],
        compiler_params=params(),
        cost_estimate=cost(10**9 if n == NF else 10**8, 10 * 10**6),
    )(r, p, w, jac, weights, *faces)


def to_coarse(r, faces, restrict, jac, weights, diag, layers):
    e_total = r.shape[0]
    span = e_total // layers
    small = weights.shape[0] // 2
    n = NC
    group = 4

    def body(r_in, h1, h2, g1, g2, rest_ref, jac_ref, w_mat, diag_ref, rc_ref, u_ref, w_ref, c1, c2, z1, z2, r_fine, count_ref):
        count_ref[...] = half_faces(n, small)
        add_halo(NF, e_total, span, lambda e: r_in[e], r_fine, h1, h2, g1, g2)

        def some(i, carry):
            first = i * group
            wide = jnp.concatenate([r_fine[first + j] for j in range(group)], axis=1)
            product = times(rest_ref[...], wide)
            for j in range(group):
                rc_ref[first + j] = product[:, j * LANES : (j + 1) * LANES]
            return carry

        lax.fori_loop(0, e_total // group, some, 0, unroll=2)

        def u_of(e, r_here):
            w_here = DAMPING / (jac_ref[pl.ds(e, 1), :] * diag_ref[...] + count_ref[...])
            w_ref[e] = w_here
            return r_here * w_here

        correct(n, e_total, span, rc_ref, u_ref, u_of, c1, c2, z1, z2)
        subtract_operator(n, e_total, span, rc_ref, u_ref, w_mat, jac_ref, count_ref)

    field = jax.ShapeDtypeStruct((e_total, small, LANES), F32)
    return pl.pallas_call(
        body,
        out_shape=[field, field, field] + face_shapes(n, layers),
        scratch_shapes=[pltpu.VMEM(r.shape, F32), pltpu.VMEM((small, LANES), F32)],
        compiler_params=params(),
        cost_estimate=cost(5 * 10**8, 5 * 10**6),
        name="to_coarse",
    )(r, *faces, restrict, jac, weights, diag)


def to_coarsest(r, faces, restrict, layers):
    e_total = r.shape[0]
    span = e_total // layers
    group = 4

    def body(r_in, h1, h2, g1, g2, rest_ref, out_ref, r_done, kept, sem):
        add_halo(NC, e_total, span, lambda e: r_in[e], r_done, h1, h2, g1, g2)

        def some(i, carry):
            first = i * group
            wide = jnp.concatenate([r_done[first + j] for j in range(group)], axis=1)
            product = times(rest_ref[...], wide)
            for j in range(group):
                kept[first + j] = product[:LAST, j * LANES : (j + 1) * LANES]
            return carry

        lax.fori_loop(0, e_total // group, some, 0, unroll=8)
        stores = []
        for e in range(e_total):
            c = pltpu.make_async_copy(kept.at[e], out_ref.at[:, e, :], sem)
            c.start()
            stores.append(c)
        for c in stores:
            c.wait()

    whole = pl.BlockSpec()
    return pl.pallas_call(
        body,
        out_shape=jax.ShapeDtypeStruct((LAST, e_total, LANES), F32),
        in_specs=[whole] * 6,
        out_specs=any_spec(),
        scratch_shapes=[
            pltpu.VMEM(r.shape, F32),
            pltpu.VMEM((e_total, LAST, LANES), F32),
            pltpu.SemaphoreType.DMA,
        ],
        compiler_params=params(),
        cost_estimate=cost(5 * 10**7, 10**6),
        name="to_coarsest",
    )(r, *faces, restrict)


def move(x, axis, by):
    count = lax.axis_size(axis)
    return lax.ppermute(x, axis, [(i, (i + by) % count) for i in range(count)])


def swap(x, axis, odd_first):
    count = lax.axis_size(axis)
    pairs = []
    for i in range(count):
        ahead = (i % 2 == 0) != odd_first
        pairs.append((i, (i + 1) % count if ahead else (i - 1) % count))
    return lax.ppermute(x, axis, pairs)


def swap_inner(x, axis, other):
    count, beside = lax.axis_size(axis), lax.axis_size(other)
    pairs = []
    for j in range(beside):
        for i in range(count):
            to = i + 1 if i % 2 else i - 1
            target = (j, to) if 0 <= to < count else (j ^ 1, i)
            pairs.append((j * count + i, target[0] * count + target[1]))
    return lax.ppermute(x, (other, axis), pairs)


def exchange(faces):
    c1, c2, z1, z2 = faces
    c2 = swap(c2, "sector", True)
    z2 = swap_inner(z2, "block", "sector")
    z1 = swap(z1, "block", False)
    c1 = swap(c1, "sector", False)
    return c1, c2, z1, z2


def windows(rotor, stator, offset, own):
    span = rotor.shape[0]
    sectors = lax.axis_size("sector")
    buckets = span // STEP
    device, rest = offset // span, offset % span

    def branch(number):
        by, bucket = number // buckets, number % buckets
        many, few = span - STEP * bucket, STEP * (bucket + 1)

        def run(rotor, stator, own):
            near = move(rotor[:many], "sector", by)
            far = move(rotor[span - few :], "sector", by + 1)
            near_s = move(stator[span - many :], "sector", -by)
            far_s = move(stator[:few], "sector", -by - 1)
            kept, w = own_part(rotor, *own)
            return *join(far, near, near_s, far_s), kept, w

        return run

    choice = device * buckets + rest // STEP
    shift = (rest % STEP).reshape(1)
    return shift, lax.switch(choice, [branch(i) for i in range(sectors * buckets)], rotor, stator, own)


def per_device(
    source, jacobian, stiff_fine, stiff_coarse, restrict_fine, restrict_coarse, mortar_proj, rotor_trace,
    stator_trace, offsets,
):
    layers, span, axial = jacobian.shape
    e_total = layers * span
    source_rows = source.reshape(source.shape[0], e_total, axial)
    jac = jacobian.reshape(e_total, axial)
    rotor_rows = rotor_trace.reshape(-1, span, axial)
    stator_rows = stator_trace.reshape(-1, span, axial)
    rotor, stator, proj, back, wf, wc, rfs, rcs, df, dc = prepare(
        rotor_rows, stator_rows, mortar_proj.transpose(1, 0, 2), stiff_fine, stiff_coarse, restrict_fine, restrict_coarse
    )
    odd = lax.axis_index("sector") % 2 == 1
    first, final = rotor[:1], rotor[span - 1 :]
    near1 = swap(jnp.where(odd, first, final), "sector", False)
    near2 = swap(jnp.where(odd, final, first), "sector", True)
    own = (near1, near2, proj, jac, df)
    shift, (rotor_win, stator_win, kept, w) = windows(rotor, stator, offsets[0], own)
    sflux, rflux, r, p, *faces = first_sweep(
        shift, rotor_win, stator_win, stator, kept, proj, back, source_rows, w, jac, wf, layers
    )
    p, r, *faces = sweep(NF, r, p, w, jac, wf, exchange(faces), layers, False)
    fine, r, *faces = sweep(NF, r, p, w, jac, wf, exchange(faces), layers, True)
    r, p, w, *faces = to_coarse(r, exchange(faces), rfs, jac, wc, dc, layers)
    p, r, *faces = sweep(NC, r, p, w, jac, wc, exchange(faces), layers, False)
    coarse, r, *faces = sweep(NC, r, p, w, jac, wc, exchange(faces), layers, True)
    coarsest = to_coarsest(r, exchange(faces), rcs, layers)
    shape = (layers, span, axial)
    return (
        sflux.reshape(stator_trace.shape),
        rflux.reshape(rotor_trace.shape),
        fine.reshape((-1,) + shape),
        coarse.reshape((-1,) + shape),
        coarsest.reshape((-1,) + shape),
    )


def solution(mesh):
    cell = P(None, None, "sector", "block")

    return jax.shard_map(
        per_device,
        mesh=mesh,
        in_specs=(cell, P(None, "sector", "block"), P(), P(), P(), P(), P(), cell, cell, P("block")),
        out_specs=(cell,) * 5,
        check_vma=False,
    )
```

profile of v0, /device:TPU:0, one launch (start us, length us, event | category | flops | bytes accessed | tf_op | source)
XLA Modules:
  0.0 105.9 jit_solution(2047557284458970494)
XLA Ops:
  0.7 2.9 %prepare.1 = (f32[16,104,128]{2,1,0:T(8,128)S(1)}, f32[16,104,128]{2,1,0:T(8,128)S(1)}, bf16[416,224]{1,0:T(8,128)(2,1)}, bf16[416,224]{1,0:T(8,128)(2,1)S(1)}, ...) custom-call(f32[100,16,128]{2,1,0:T(8,128)} %bitcast.17, ...), custom_call_target="tpu_custom_call" | custom-call | tf_op jit(solution)/shard_map/prepare/pallas_call | solution.py:261
  3.6 3.4 %collective-permute-start.129 = (f32[1,104,128]{2,1,0:T(8,128)S(1)}, f32[1,104,128]{2,1,0:T(8,128)S(1)}, u32[]{:S(2)}, u32[]{:S(2)}) collective-permute-start(f32[1,104,128]{2,1,0:T(8,128)S(1)} %get-tuple-element.911), channel_id=1, source_target_pairs={{0,28},{4,8},{8,4},{12,16},{16,12},{20,24},{24,20},{28,0},{1,29},{... | collective-permute-start | bytes 159752 | tf_op jit(solution)/shard_map/ppermute | solution.py:578
  7.8 1.1 %collective-permute-done.129 = f32[1,104,128]{2,1,0:T(8,128)S(1)} collective-permute-done((f32[1,104,128]{2,1,0:T(8,128)S(1)}, f32[1,104,128]{2,1,0:T(8,128)S(1)}, u32[]{:S(2)}, u32[]{:S(2)}) %collective-permute-start.129) | collective-permute-done | bytes 53280 | tf_op jit(solution)/shard_map/ppermute | solution.py:578
  8.9 12.6 %conditional.1 = (f32[20,104,128]{2,1,0:T(8,128)S(1)}, f32[20,104,128]{2,1,0:T(8,128)S(1)}, f32[17,104,128]{2,1,0:T(8,128)}, f32[32,128,128]{2,1,0:T(8,128)}) conditional(s32[]{:T(128)} %clamp.3, (f32[16,104,128]{2,1,0:T(8,128)S(1)}, f32[16,104,128]{2,1,0:T(8,128)S(1)}, f32[1,104,128]{2,1,0:T(8,128)S(1)}, ...), branch_computations={%region_0.1_spmd, %region_1.2_spmd, %region_2.3_spmd, %region_3.4_... | conditional | flops 2000000000 | bytes 23205752 | solution.py:623
  8.9 0.6 copy-done.2
  9.5 0.0 collective-permute-start.5
  9.6 0.0 copy-start.3
  9.7 0.0 collective-permute-start.6
  9.7 0.1 collective-permute-start.4
  9.8 2.7 %collective-permute-start.7 = (f32[8,104,128]{2,1,0:T(8,128)S(1)}, f32[8,104,128]{2,1,0:T(8,128)S(1)}, u32[]{:S(2)}, u32[]{:S(2)}) collective-permute-start(f32[8,104,128]{2,1,0:T(8,128)S(1)} %slice.201), channel_id=1, source_target_pairs={{0,28},{4,0},{8,4},{12,8},{16,12},{20,16},{24,20},{28,24},{1,29},{... | collective-permute-start | bytes 1277960 | tf_op jit(solution)/shard_map/cond/branch_1_fun/ppermute | solution.py:569
  12.5 4.8 %own_part.33 = (f32[17,104,128]{2,1,0:T(8,128)}, f32[32,128,128]{2,1,0:T(8,128)}) custom-call(f32[16,104,128]{2,1,0:T(8,128)S(1)} %get-tuple-element.459.r_in, f32[1,104,128]{2,1,0:T(8,128)S(1)} %copy-done.3, f32[1,104,128]{2,1,0:T(8,128)S(1)} %get-tuple-element.464.near2_ref, bf16[416,224]{1,0:T(8,128)(2,1)} %get-tuple-element.465.proj_ref, ...), custom_call_target="tpu_custom_call" | custom-call | flops 2000000000 | bytes 10000000 | tf_op jit(solution)/shard_map/cond/branch_1_fun/own_part/pallas_call | solution.py:333
  17.4 3.1 %collective-permute-done.4.far_ref = f32[8,104,128]{2,1,0:T(8,128)S(1)} collective-permute-done((f32[8,104,128]{2,1,0:T(8,128)S(1)}, f32[8,104,128]{2,1,0:T(8,128)S(1)}, u32[]{:S(2)}, u32[]{:S(2)}) %collective-permute-start.4) | collective-permute-done | bytes 426016 | tf_op jit(solution)/shard_map/cond/branch_1_fun/ppermute | solution.py:569
  20.5 0.3 collective-permute-done.7.far_s_ref
  20.8 0.2 join.33
  21.5 7.5 %first_sweep.1 = (f32[100,16,128]{2,1,0:T(8,128)}, f32[100,16,128]{2,1,0:T(8,128)}, f32[32,128,128]{2,1,0:T(8,128)S(1)}, f32[32,128,128]{2,1,0:T(8,128)S(1)}, f3...) custom-call(s32[1]{0:T(128)} %bitcast.1.shift_ref, ...), custom_call_target="tpu_custom_call" | custom-call | flops 2000000000 | bytes 20000000 | tf_op jit(solution)/shard_map/first_sweep/pallas_call | solution.py:422
  29.0 2.7 %collective-permute-start.130 = (f32[2,25,128]{2,1,0:T(8,128)S(1)}, f32[2,25,128]{2,1,0:T(8,128)S(1)}, u32[]{:S(2)}, u32[]{:S(2)}) collective-permute-start(f32[2,25,128]{2,1,0:T(8,128)S(1)} %get-tuple-element.872), channel_id=1, source_target_pairs={{0,4},{4,0},{8,12},{12,8},{16,20},{20,16},{24,28},{28,24},{1,5},{5... | collective-permute-start | bytes 76808 | tf_op jit(solution)/shard_map/ppermute | solution.py:578
  31.7 0.2 collective-permute-start.131
  31.9 33.6 %collective-permute-start.132 = (f32[5,8,128]{2,1,0:T(8,128)S(1)}, f32[5,8,128]{2,1,0:T(8,128)S(1)}, u32[]{:S(2)}, u32[]{:S(2)}) collective-permute-start(f32[5,8,128]{2,1,0:T(8,128)S(1)} %get-tuple-element.874), channel_id=1, source_target_pairs={{0,1},{1,0},{2,3},{3,2},{4,5},{5,4},{6,7},{7,6},{8,9},{9,8},{10,11... | collective-permute-start | bytes 61448 | tf_op jit(solution)/shard_map/ppermute | solution.py:578
  65.5 1.8 %collective-permute-done.132.g1 = f32[5,8,128]{2,1,0:T(8,128)S(1)} collective-permute-done((f32[5,8,128]{2,1,0:T(8,128)S(1)}, f32[5,8,128]{2,1,0:T(8,128)S(1)}, u32[]{:S(2)}, u32[]{:S(2)}) %collective-permute-start.132) | collective-permute-done | bytes 20512 | tf_op jit(solution)/shard_map/ppermute | solution.py:578
  67.3 2.4 %shard_map.137 = (f32[32,128,128]{2,1,0:T(8,128)S(1)}, f32[32,128,128]{2,1,0:T(8,128)S(1)}, f32[2,25,128]{2,1,0:T(8,128)S(1)}, f32[2,25,128]{2,1,0:T(8,128)S(1)}...) custom-call(f32[32,128,128]{2,1,0:T(8,128)S(1)} %get-tuple-element.870.r_in, ...), custom_call_target="tpu_custom_call" | custom-call | flops 1000000000 | bytes 10000000 | tf_op jit(solution)/shard_map/pallas_call | solution.py:470
  69.7 0.1 collective-permute-start.134
  69.8 0.7 collective-permute-start.135
  70.4 2.0 %collective-permute-start.136 = (f32[5,8,128]{2,1,0:T(8,128)S(1)}, f32[5,8,128]{2,1,0:T(8,128)S(1)}, u32[]{:S(2)}, u32[]{:S(2)}) collective-permute-start(f32[5,8,128]{2,1,0:T(8,128)S(1)} %get-tuple-element.880), channel_id=1, source_target_pairs={{0,1},{1,0},{2,3},{3,2},{4,5},{5,4},{6,7},{7,6},{8,9},{9,8},{10,11... | collective-permute-start | bytes 61448 | tf_op jit(solution)/shard_map/ppermute | solution.py:578
  72.5 1.8 %collective-permute-done.136.g1 = f32[5,8,128]{2,1,0:T(8,128)S(1)} collective-permute-done((f32[5,8,128]{2,1,0:T(8,128)S(1)}, f32[5,8,128]{2,1,0:T(8,128)S(1)}, u32[]{:S(2)}, u32[]{:S(2)}) %collective-permute-start.136) | collective-permute-done | bytes 20512 | tf_op jit(solution)/shard_map/ppermute | solution.py:578
  74.2 2.4 %shard_map.138 = (f32[125,32,128]{2,1,0:T(8,128)}, f32[32,128,128]{2,1,0:T(8,128)S(1)}, f32[2,25,128]{2,1,0:T(8,128)S(1)}, f32[2,25,128]{2,1,0:T(8,128)S(1)}, f3...) custom-call(f32[32,128,128]{2,1,0:T(8,128)S(1)} %get-tuple-element.876.r_in, ...), custom_call_target="tpu_custom_call" | custom-call | flops 1000000000 | bytes 10000000 | tf_op jit(solution)/shard_map/pallas_call | solution.py:470
  76.7 0.1 collective-permute-start.138
  76.7 1.5 %collective-permute-start.139 = (f32[2,25,128]{2,1,0:T(8,128)S(1)}, f32[2,25,128]{2,1,0:T(8,128)S(1)}, u32[]{:S(2)}, u32[]{:S(2)}) collective-permute-start(f32[2,25,128]{2,1,0:T(8,128)S(1)} %get-tuple-element.885), channel_id=1, source_target_pairs={{0,28},{4,8},{8,4},{12,16},{16,12},{20,24},{24,20},{28,0},{1,29},{... | collective-permute-start | bytes 76808 | tf_op jit(solution)/shard_map/ppermute | solution.py:578
  78.2 2.2 %collective-permute-start.140 = (f32[5,8,128]{2,1,0:T(8,128)S(1)}, f32[5,8,128]{2,1,0:T(8,128)S(1)}, u32[]{:S(2)}, u32[]{:S(2)}) collective-permute-start(f32[5,8,128]{2,1,0:T(8,128)S(1)} %get-tuple-element.886), channel_id=1, source_target_pairs={{0,1},{1,0},{2,3},{3,2},{4,5},{5,4},{6,7},{7,6},{8,9},{9,8},{10,11... | collective-permute-start | bytes 61448 | tf_op jit(solution)/shard_map/ppermute | solution.py:578
  80.4 1.8 %collective-permute-done.140.g1 = f32[5,8,128]{2,1,0:T(8,128)S(1)} collective-permute-done((f32[5,8,128]{2,1,0:T(8,128)S(1)}, f32[5,8,128]{2,1,0:T(8,128)S(1)}, u32[]{:S(2)}, u32[]{:S(2)}) %collective-permute-start.140) | collective-permute-done | bytes 20512 | tf_op jit(solution)/shard_map/ppermute | solution.py:578
  82.2 2.2 %to_coarse.1 = (f32[32,32,128]{2,1,0:T(8,128)S(1)}, f32[32,32,128]{2,1,0:T(8,128)S(1)}, f32[32,32,128]{2,1,0:T(8,128)S(1)}, f32[2,9,128]{2,1,0:T(8,128)S(1)}, f3...) custom-call(f32[32,128,128]{2,1,0:T(8,128)S(1)} %get-tuple-element.883.r_in, ...), custom_call_target="tpu_custom_call" | custom-call | flops 500000000 | bytes 5000000 | tf_op jit(solution)/shard_map/to_coarse/pallas_call | solution.py:515
  84.4 2.1 %collective-permute-start.144 = (f32[3,8,128]{2,1,0:T(8,128)S(1)}, f32[3,8,128]{2,1,0:T(8,128)S(1)}, u32[]{:S(2)}, u32[]{:S(2)}) collective-permute-start(f32[3,8,128]{2,1,0:T(8,128)S(1)} %get-tuple-element.896), channel_id=1, source_target_pairs={{0,1},{1,0},{2,3},{3,2},{4,5},{5,4},{6,7},{7,6},{8,9},{9,8},{10,11... | collective-permute-start | bytes 36872 | tf_op jit(solution)/shard_map/ppermute | solution.py:578
  86.5 0.5 collective-permute-start.142
  87.0 0.3 collective-permute-start.143
  87.3 0.5 collective-permute-done.142.h1
  87.9 3.3 %collective-permute-done.143.h2 = f32[2,9,128]{2,1,0:T(8,128)S(1)} collective-permute-done((f32[2,9,128]{2,1,0:T(8,128)S(1)}, f32[2,9,128]{2,1,0:T(8,128)S(1)}, u32[]{:S(2)}, u32[]{:S(2)}) %collective-permute-start.143) | collective-permute-done | bytes 9248 | tf_op jit(solution)/shard_map/ppermute | solution.py:578
  91.2 1.2 %shard_map.139 = (f32[32,32,128]{2,1,0:T(8,128)S(1)}, f32[32,32,128]{2,1,0:T(8,128)S(1)}, f32[2,9,128]{2,1,0:T(8,128)S(1)}, f32[2,9,128]{2,1,0:T(8,128)S(1)}, f3...) custom-call(f32[32,32,128]{2,1,0:T(8,128)S(1)} %get-tuple-element.891.r_in, f32[32,32,128]{2,1,0:T(8,128)S(1)} %get-tuple-element.892.p_in, ...), custom_call_target="tpu_custom_call" | custom-call | flops 100000000 | bytes 10000000 | tf_op jit(solution)/shard_map/pallas_call | solution.py:470
  92.4 0.1 collective-permute-start.148
  92.5 0.1 collective-permute-start.149
  92.5 0.5 collective-permute-start.146
  93.0 0.2 collective-permute-start.147
  93.2 0.7 collective-permute-done.146.h1
  93.9 3.4 %collective-permute-done.147.h2 = f32[2,9,128]{2,1,0:T(8,128)S(1)} collective-permute-done((f32[2,9,128]{2,1,0:T(8,128)S(1)}, f32[2,9,128]{2,1,0:T(8,128)S(1)}, u32[]{:S(2)}, u32[]{:S(2)}) %collective-permute-start.147) | collective-permute-done | bytes 9248 | tf_op jit(solution)/shard_map/ppermute | solution.py:578
  97.2 1.2 %shard_map.140 = (f32[27,32,128]{2,1,0:T(8,128)}, f32[32,32,128]{2,1,0:T(8,128)S(1)}, f32[2,9,128]{2,1,0:T(8,128)S(1)}, f32[2,9,128]{2,1,0:T(8,128)S(1)}, f32[3,...) custom-call(f32[32,32,128]{2,1,0:T(8,128)S(1)} %get-tuple-element.898.r_in, f32[32,32,128]{2,1,0:T(8,128)S(1)} %get-tuple-element.899.p_in, ...), custom_call_target="tpu_custom_call" | custom-call | flops 100000000 | bytes 10000000 | tf_op jit(solution)/shard_map/pallas_call | solution.py:470
  98.5 1.4 %collective-permute-start.152 = (f32[3,8,128]{2,1,0:T(8,128)S(1)}, f32[3,8,128]{2,1,0:T(8,128)S(1)}, u32[]{:S(2)}, u32[]{:S(2)}) collective-permute-start(f32[3,8,128]{2,1,0:T(8,128)S(1)} %get-tuple-element.908), channel_id=1, source_target_pairs={{0,1},{1,0},{2,3},{3,2},{4,5},{5,4},{6,7},{7,6},{8,9},{9,8},{10,11... | collective-permute-start | bytes 36872 | tf_op jit(solution)/shard_map/ppermute | solution.py:578
  99.8 0.5 collective-permute-start.150
  100.4 0.8 collective-permute-done.150.h1
  101.2 3.3 %collective-permute-done.151.h2 = f32[2,9,128]{2,1,0:T(8,128)S(1)} collective-permute-done((f32[2,9,128]{2,1,0:T(8,128)S(1)}, f32[2,9,128]{2,1,0:T(8,128)S(1)}, u32[]{:S(2)}, u32[]{:S(2)}) %collective-permute-start.151) | collective-permute-done | bytes 9248 | tf_op jit(solution)/shard_map/ppermute | solution.py:578
  104.5 1.2 %to_coarsest.1 = f32[8,32,128]{2,1,0:T(8,128)} custom-call(f32[32,32,128]{2,1,0:T(8,128)S(1)} %get-tuple-element.905.r_in, f32[2,9,128]{2,1,0:T(8,128)S(1)} %collective-permute-done.150.h1, f32[2,9,128]{2,1,0:T(8,128)S(1)} %collective-permute-done.151.h2, f32[3,8,128]{2,1,0:T(8,128)S(1)} %collective-permute-done.152.g1, ...), custom_call_target="tpu_custom_call" | custom-call | flops 50000000 | bytes 1000000 | tf_op jit(solution)/shard_map/to_coarsest/pallas_call | solution.py:551
  (36 shorter events, 0.2 us)
Async XLA Ops:
  0.6 8.2 %copy-start.1 = (f32[2,16,128]{2,1,0:T(8,128)S(1)}, f32[2,16,128]{2,1,0:T(8,128)}, u32[]{:S(2)}) copy-start(f32[2,16,128]{2,1,0:T(8,128)} %param.43) | copy-start | bytes 49156
  3.6 5.2 %collective-permute-start.129 = (f32[1,104,128]{2,1,0:T(8,128)S(1)}, f32[1,104,128]{2,1,0:T(8,128)S(1)}, u32[]{:S(2)}, u32[]{:S(2)}) collective-permute-start(f32[1,104,128]{2,1,0:T(8,128)S(1)} %get-tuple-element.911), channel_id=1, source_target_pairs={{0,28},{4,8},{8,4},{12,16},{16,12},{20,24},{24,20},{28,0},{1,29},{... | collective-permute-start | bytes 159752 | tf_op jit(solution)/shard_map/ppermute | solution.py:578
  7.0 1.8 %collective-permute-start.128 = (f32[1,104,128]{2,1,0:T(8,128)S(1)}, f32[1,104,128]{2,1,0:T(8,128)S(1)}, u32[]{:S(2)}, u32[]{:S(2)}) collective-permute-start(f32[1,104,128]{2,1,0:T(8,128)S(1)} %get-tuple-element.912), channel_id=1, source_target_pairs={{0,4},{4,0},{8,12},{12,8},{16,20},{20,16},{24,28},{28,24},{1,5},{5... | collective-permute-start | bytes 159752 | tf_op jit(solution)/shard_map/ppermute | solution.py:578
  8.9 0.6 copy-start.2
  9.5 11.2 %collective-permute-start.5 = (f32[12,104,128]{2,1,0:T(8,128)S(1)}, f32[12,104,128]{2,1,0:T(8,128)S(1)}, u32[]{:S(2)}, u32[]{:S(2)}) collective-permute-start(f32[12,104,128]{2,1,0:T(8,128)S(1)} %slice.199), channel_id=1, source_target_pairs={{0,0},{4,4},{8,8},{12,12},{16,16},{20,20},{24,24},{28,28},{1,1},{5... | collective-permute-start | bytes 1916936 | tf_op jit(solution)/shard_map/cond/branch_1_fun/ppermute | solution.py:569
  9.6 2.9 %copy-start.3 = (f32[1,104,128]{2,1,0:T(8,128)S(1)}, f32[1,104,128]{2,1,0:T(8,128)}, u32[]{:S(2)}) copy-start(f32[1,104,128]{2,1,0:T(8,128)} %copy-done.2) | copy-start | bytes 159748 | tf_op jit(solution)/shard_map/cond
  9.7 11.1 %collective-permute-start.6 = (f32[12,104,128]{2,1,0:T(8,128)S(1)}, f32[12,104,128]{2,1,0:T(8,128)S(1)}, u32[]{:S(2)}, u32[]{:S(2)}) collective-permute-start(f32[12,104,128]{2,1,0:T(8,128)S(1)} %slice.200), channel_id=1, source_target_pairs={{0,0},{4,4},{8,8},{12,12},{16,16},{20,20},{24,24},{28,28},{1,1},{5... | collective-permute-start | bytes 1916936 | tf_op jit(solution)/shard_map/cond/branch_1_fun/ppermute | solution.py:569
  9.7 10.8 %collective-permute-start.4 = (f32[8,104,128]{2,1,0:T(8,128)S(1)}, f32[8,104,128]{2,1,0:T(8,128)S(1)}, u32[]{:S(2)}, u32[]{:S(2)}) collective-permute-start(f32[8,104,128]{2,1,0:T(8,128)S(1)} %slice.198), channel_id=1, source_target_pairs={{0,4},{4,8},{8,12},{12,16},{16,20},{20,24},{24,28},{28,0},{1,5},{5... | collective-permute-start | bytes 1277960 | tf_op jit(solution)/shard_map/cond/branch_1_fun/ppermute | solution.py:569
  9.8 10.9 %collective-permute-start.7 = (f32[8,104,128]{2,1,0:T(8,128)S(1)}, f32[8,104,128]{2,1,0:T(8,128)S(1)}, u32[]{:S(2)}, u32[]{:S(2)}) collective-permute-start(f32[8,104,128]{2,1,0:T(8,128)S(1)} %slice.201), channel_id=1, source_target_pairs={{0,28},{4,0},{8,4},{12,8},{16,12},{20,16},{24,20},{28,24},{1,29},{... | collective-permute-start | bytes 1277960 | tf_op jit(solution)/shard_map/cond/branch_1_fun/ppermute | solution.py:569
  21.5 45.8 %copy-start = (f32[32,128,128]{2,1,0:T(8,128)S(1)}, f32[32,128,128]{2,1,0:T(8,128)}, u32[]{:S(2)}) copy-start(f32[32,128,128]{2,1,0:T(8,128)} %get-tuple-element.866.w_ref.w_in) | copy-start | bytes 6291460
  29.0 38.3 %collective-permute-start.130 = (f32[2,25,128]{2,1,0:T(8,128)S(1)}, f32[2,25,128]{2,1,0:T(8,128)S(1)}, u32[]{:S(2)}, u32[]{:S(2)}) collective-permute-start(f32[2,25,128]{2,1,0:T(8,128)S(1)} %get-tuple-element.872), channel_id=1, source_target_pairs={{0,4},{4,0},{8,12},{12,8},{16,20},{20,16},{24,28},{28,24},{1,5},{5... | collective-permute-start | bytes 76808 | tf_op jit(solution)/shard_map/ppermute | solution.py:578
  31.7 35.6 %collective-permute-start.131 = (f32[2,25,128]{2,1,0:T(8,128)S(1)}, f32[2,25,128]{2,1,0:T(8,128)S(1)}, u32[]{:S(2)}, u32[]{:S(2)}) collective-permute-start(f32[2,25,128]{2,1,0:T(8,128)S(1)} %get-tuple-element.873), channel_id=1, source_target_pairs={{0,28},{4,8},{8,4},{12,16},{16,12},{20,24},{24,20},{28,0},{1,29},{... | collective-permute-start | bytes 76808 | tf_op jit(solution)/shard_map/ppermute | solution.py:578
  31.9 35.3 %collective-permute-start.132 = (f32[5,8,128]{2,1,0:T(8,128)S(1)}, f32[5,8,128]{2,1,0:T(8,128)S(1)}, u32[]{:S(2)}, u32[]{:S(2)}) collective-permute-start(f32[5,8,128]{2,1,0:T(8,128)S(1)} %get-tuple-element.874), channel_id=1, source_target_pairs={{0,1},{1,0},{2,3},{3,2},{4,5},{5,4},{6,7},{7,6},{8,9},{9,8},{10,11... | collective-permute-start | bytes 61448 | tf_op jit(solution)/shard_map/ppermute | solution.py:578
  65.5 1.8 %collective-permute-start.133 = (f32[5,8,128]{2,1,0:T(8,128)S(1)}, f32[5,8,128]{2,1,0:T(8,128)S(1)}, u32[]{:S(2)}, u32[]{:S(2)}) collective-permute-start(f32[5,8,128]{2,1,0:T(8,128)S(1)} %get-tuple-element.875), channel_id=1, source_target_pairs={{0,4},{1,2},{2,1},{3,7},{4,0},{5,6},{6,5},{7,3},{8,12},{9,10},{10,... | collective-permute-start | bytes 61448 | tf_op jit(solution)/shard_map/ppermute | solution.py:589
  69.7 4.5 %collective-permute-start.134 = (f32[2,25,128]{2,1,0:T(8,128)S(1)}, f32[2,25,128]{2,1,0:T(8,128)S(1)}, u32[]{:S(2)}, u32[]{:S(2)}) collective-permute-start(f32[2,25,128]{2,1,0:T(8,128)S(1)} %get-tuple-element.878), channel_id=1, source_target_pairs={{0,4},{4,0},{8,12},{12,8},{16,20},{20,16},{24,28},{28,24},{1,5},{5... | collective-permute-start | bytes 76808 | tf_op jit(solution)/shard_map/ppermute | solution.py:578
  69.8 4.5 %collective-permute-start.135 = (f32[2,25,128]{2,1,0:T(8,128)S(1)}, f32[2,25,128]{2,1,0:T(8,128)S(1)}, u32[]{:S(2)}, u32[]{:S(2)}) collective-permute-start(f32[2,25,128]{2,1,0:T(8,128)S(1)} %get-tuple-element.879), channel_id=1, source_target_pairs={{0,28},{4,8},{8,4},{12,16},{16,12},{20,24},{24,20},{28,0},{1,29},{... | collective-permute-start | bytes 76808 | tf_op jit(solution)/shard_map/ppermute | solution.py:578
  70.4 3.8 %collective-permute-start.136 = (f32[5,8,128]{2,1,0:T(8,128)S(1)}, f32[5,8,128]{2,1,0:T(8,128)S(1)}, u32[]{:S(2)}, u32[]{:S(2)}) collective-permute-start(f32[5,8,128]{2,1,0:T(8,128)S(1)} %get-tuple-element.880), channel_id=1, source_target_pairs={{0,1},{1,0},{2,3},{3,2},{4,5},{5,4},{6,7},{7,6},{8,9},{9,8},{10,11... | collective-permute-start | bytes 61448 | tf_op jit(solution)/shard_map/ppermute | solution.py:578
  72.5 1.8 %collective-permute-start.137 = (f32[5,8,128]{2,1,0:T(8,128)S(1)}, f32[5,8,128]{2,1,0:T(8,128)S(1)}, u32[]{:S(2)}, u32[]{:S(2)}) collective-permute-start(f32[5,8,128]{2,1,0:T(8,128)S(1)} %get-tuple-element.881), channel_id=1, source_target_pairs={{0,4},{1,2},{2,1},{3,7},{4,0},{5,6},{6,5},{7,3},{8,12},{9,10},{10,... | collective-permute-start | bytes 61448 | tf_op jit(solution)/shard_map/ppermute | solution.py:589
  76.7 5.5 %collective-permute-start.138 = (f32[2,25,128]{2,1,0:T(8,128)S(1)}, f32[2,25,128]{2,1,0:T(8,128)S(1)}, u32[]{:S(2)}, u32[]{:S(2)}) collective-permute-start(f32[2,25,128]{2,1,0:T(8,128)S(1)} %get-tuple-element.884), channel_id=1, source_target_pairs={{0,4},{4,0},{8,12},{12,8},{16,20},{20,16},{24,28},{28,24},{1,5},{5... | collective-permute-start | bytes 76808 | tf_op jit(solution)/shard_map/ppermute | solution.py:578
  76.7 5.5 %collective-permute-start.139 = (f32[2,25,128]{2,1,0:T(8,128)S(1)}, f32[2,25,128]{2,1,0:T(8,128)S(1)}, u32[]{:S(2)}, u32[]{:S(2)}) collective-permute-start(f32[2,25,128]{2,1,0:T(8,128)S(1)} %get-tuple-element.885), channel_id=1, source_target_pairs={{0,28},{4,8},{8,4},{12,16},{16,12},{20,24},{24,20},{28,0},{1,29},{... | collective-permute-start | bytes 76808 | tf_op jit(solution)/shard_map/ppermute | solution.py:578
  78.2 3.9 %collective-permute-start.140 = (f32[5,8,128]{2,1,0:T(8,128)S(1)}, f32[5,8,128]{2,1,0:T(8,128)S(1)}, u32[]{:S(2)}, u32[]{:S(2)}) collective-permute-start(f32[5,8,128]{2,1,0:T(8,128)S(1)} %get-tuple-element.886), channel_id=1, source_target_pairs={{0,1},{1,0},{2,3},{3,2},{4,5},{5,4},{6,7},{7,6},{8,9},{9,8},{10,11... | collective-permute-start | bytes 61448 | tf_op jit(solution)/shard_map/ppermute | solution.py:578
  80.4 1.8 %collective-permute-start.141 = (f32[5,8,128]{2,1,0:T(8,128)S(1)}, f32[5,8,128]{2,1,0:T(8,128)S(1)}, u32[]{:S(2)}, u32[]{:S(2)}) collective-permute-start(f32[5,8,128]{2,1,0:T(8,128)S(1)} %get-tuple-element.887), channel_id=1, source_target_pairs={{0,4},{1,2},{2,1},{3,7},{4,0},{5,6},{6,5},{7,3},{8,12},{9,10},{10,... | collective-permute-start | bytes 61448 | tf_op jit(solution)/shard_map/ppermute | solution.py:589
  84.4 6.8 %collective-permute-start.144 = (f32[3,8,128]{2,1,0:T(8,128)S(1)}, f32[3,8,128]{2,1,0:T(8,128)S(1)}, u32[]{:S(2)}, u32[]{:S(2)}) collective-permute-start(f32[3,8,128]{2,1,0:T(8,128)S(1)} %get-tuple-element.896), channel_id=1, source_target_pairs={{0,1},{1,0},{2,3},{3,2},{4,5},{5,4},{6,7},{7,6},{8,9},{9,8},{10,11... | collective-permute-start | bytes 36872 | tf_op jit(solution)/shard_map/ppermute | solution.py:578
  86.5 4.7 %collective-permute-start.145 = (f32[3,8,128]{2,1,0:T(8,128)S(1)}, f32[3,8,128]{2,1,0:T(8,128)S(1)}, u32[]{:S(2)}, u32[]{:S(2)}) collective-permute-start(f32[3,8,128]{2,1,0:T(8,128)S(1)} %get-tuple-element.897), channel_id=1, source_target_pairs={{0,4},{1,2},{2,1},{3,7},{4,0},{5,6},{6,5},{7,3},{8,12},{9,10},{10,... | collective-permute-start | bytes 36872 | tf_op jit(solution)/shard_map/ppermute | solution.py:589
  86.5 1.3 %collective-permute-start.142 = (f32[2,9,128]{2,1,0:T(8,128)S(1)}, f32[2,9,128]{2,1,0:T(8,128)S(1)}, u32[]{:S(2)}, u32[]{:S(2)}) collective-permute-start(f32[2,9,128]{2,1,0:T(8,128)S(1)} %get-tuple-element.894), channel_id=1, source_target_pairs={{0,4},{4,0},{8,12},{12,8},{16,20},{20,16},{24,28},{28,24},{1,5},{5... | collective-permute-start | bytes 27656 | tf_op jit(solution)/shard_map/ppermute | solution.py:578
  87.0 4.2 %collective-permute-start.143 = (f32[2,9,128]{2,1,0:T(8,128)S(1)}, f32[2,9,128]{2,1,0:T(8,128)S(1)}, u32[]{:S(2)}, u32[]{:S(2)}) collective-permute-start(f32[2,9,128]{2,1,0:T(8,128)S(1)} %get-tuple-element.895), channel_id=1, source_target_pairs={{0,28},{4,8},{8,4},{12,16},{16,12},{20,24},{24,20},{28,0},{1,29},{... | collective-permute-start | bytes 27656 | tf_op jit(solution)/shard_map/ppermute | solution.py:578
  92.4 4.9 %collective-permute-start.148 = (f32[3,8,128]{2,1,0:T(8,128)S(1)}, f32[3,8,128]{2,1,0:T(8,128)S(1)}, u32[]{:S(2)}, u32[]{:S(2)}) collective-permute-start(f32[3,8,128]{2,1,0:T(8,128)S(1)} %get-tuple-element.902), channel_id=1, source_target_pairs={{0,1},{1,0},{2,3},{3,2},{4,5},{5,4},{6,7},{7,6},{8,9},{9,8},{10,11... | collective-permute-start | bytes 36872 | tf_op jit(solution)/shard_map/ppermute | solution.py:578
  92.5 4.8 %collective-permute-start.149 = (f32[3,8,128]{2,1,0:T(8,128)S(1)}, f32[3,8,128]{2,1,0:T(8,128)S(1)}, u32[]{:S(2)}, u32[]{:S(2)}) collective-permute-start(f32[3,8,128]{2,1,0:T(8,128)S(1)} %get-tuple-element.903), channel_id=1, source_target_pairs={{0,4},{1,2},{2,1},{3,7},{4,0},{5,6},{6,5},{7,3},{8,12},{9,10},{10,... | collective-permute-start | bytes 36872 | tf_op jit(solution)/shard_map/ppermute | solution.py:589
  92.5 1.3 %collective-permute-start.146 = (f32[2,9,128]{2,1,0:T(8,128)S(1)}, f32[2,9,128]{2,1,0:T(8,128)S(1)}, u32[]{:S(2)}, u32[]{:S(2)}) collective-permute-start(f32[2,9,128]{2,1,0:T(8,128)S(1)} %get-tuple-element.900), channel_id=1, source_target_pairs={{0,4},{4,0},{8,12},{12,8},{16,20},{20,16},{24,28},{28,24},{1,5},{5... | collective-permute-start | bytes 27656 | tf_op jit(solution)/shard_map/ppermute | solution.py:578
  93.0 4.2 %collective-permute-start.147 = (f32[2,9,128]{2,1,0:T(8,128)S(1)}, f32[2,9,128]{2,1,0:T(8,128)S(1)}, u32[]{:S(2)}, u32[]{:S(2)}) collective-permute-start(f32[2,9,128]{2,1,0:T(8,128)S(1)} %get-tuple-element.901), channel_id=1, source_target_pairs={{0,28},{4,8},{8,4},{12,16},{16,12},{20,24},{24,20},{28,0},{1,29},{... | collective-permute-start | bytes 27656 | tf_op jit(solution)/shard_map/ppermute | solution.py:578
  98.5 6.0 %collective-permute-start.152 = (f32[3,8,128]{2,1,0:T(8,128)S(1)}, f32[3,8,128]{2,1,0:T(8,128)S(1)}, u32[]{:S(2)}, u32[]{:S(2)}) collective-permute-start(f32[3,8,128]{2,1,0:T(8,128)S(1)} %get-tuple-element.908), channel_id=1, source_target_pairs={{0,1},{1,0},{2,3},{3,2},{4,5},{5,4},{6,7},{7,6},{8,9},{9,8},{10,11... | collective-permute-start | bytes 36872 | tf_op jit(solution)/shard_map/ppermute | solution.py:578
  99.8 4.6 %collective-permute-start.153 = (f32[3,8,128]{2,1,0:T(8,128)S(1)}, f32[3,8,128]{2,1,0:T(8,128)S(1)}, u32[]{:S(2)}, u32[]{:S(2)}) collective-permute-start(f32[3,8,128]{2,1,0:T(8,128)S(1)} %get-tuple-element.909), channel_id=1, source_target_pairs={{0,4},{1,2},{2,1},{3,7},{4,0},{5,6},{6,5},{7,3},{8,12},{9,10},{10,... | collective-permute-start | bytes 36872 | tf_op jit(solution)/shard_map/ppermute | solution.py:589
  99.8 1.3 %collective-permute-start.150 = (f32[2,9,128]{2,1,0:T(8,128)S(1)}, f32[2,9,128]{2,1,0:T(8,128)S(1)}, u32[]{:S(2)}, u32[]{:S(2)}) collective-permute-start(f32[2,9,128]{2,1,0:T(8,128)S(1)} %get-tuple-element.906), channel_id=1, source_target_pairs={{0,4},{4,0},{8,12},{12,8},{16,20},{20,16},{24,28},{28,24},{1,5},{5... | collective-permute-start | bytes 27656 | tf_op jit(solution)/shard_map/ppermute | solution.py:578
  100.4 4.1 %collective-permute-start.151 = (f32[2,9,128]{2,1,0:T(8,128)S(1)}, f32[2,9,128]{2,1,0:T(8,128)S(1)}, u32[]{:S(2)}, u32[]{:S(2)}) collective-permute-start(f32[2,9,128]{2,1,0:T(8,128)S(1)} %get-tuple-element.907), channel_id=1, source_target_pairs={{0,28},{4,8},{8,4},{12,16},{16,12},{20,24},{24,20},{28,0},{1,29},{... | collective-permute-start | bytes 27656 | tf_op jit(solution)/shard_map/ppermute | solution.py:578
where the time goes:
time: 106 us
  starting transfers between devices  54.9 us (52%)
  Pallas kernels  26.2 us (25%)
  waiting for transfers between devices  21.8 us (21%)
  between operations  1.7 us (2%)
    ppermute x20, starting transfers between devices, swap(): return lax.ppermute(x, axis, pairs)  52 us
    ppermute x20, waiting for transfers between devices, swap(): return lax.ppermute(x, axis, pairs)  18.4 us
    pallas_call x1, Pallas kernels, first_sweep(): pl.pallas_call(body, out_shape=[trace, trace, field, field] + face_shapes...  7.5 us
    pallas_call x4, Pallas kernels, sweep(): pl.pallas_call(body, out_shape=[kept, field] + face_shapes(n, layers), ou...  7.2 us
    pallas_call x1, Pallas kernels, own_part(): pl.pallas_call(body, out_shape=[jax.ShapeDtypeStruct((span + 1, tall, LAN...  4.84 us
    ppermute x4, waiting for transfers between devices, move(): return lax.ppermute(x, axis, [(i, (i + by) % count) for i in range(count)])  3.4 us
    pallas_call x1, Pallas kernels, prepare(): pl.pallas_call(body, out_shape=[jax.ShapeDtypeStruct((span, tall, LANES),...  2.94 us
    ppermute x4, starting transfers between devices, move(): return lax.ppermute(x, axis, [(i, (i + by) % count) for i in range(count)])  2.84 us
  transfers between devices with their start and end apart: 30, of which 12 were waited for; matrix products, arithmetic and copies ran while one was open for 0% of the time, Pallas kernels for 5%

commit v1 on v0

--- a/solution.py
+++ b/solution.py
@@ -15,7 +15,7 @@
 NC = 3
 LAST = 8
 STEP = 4
-FACE_UNROLL = 5
+SUM_ROWS = 32
 HALO_UNROLL = 32
 GROUP = {NF: 4, NC: 16}
 GROUP_UNROLL = {NF: 4, NC: 1}
@@ -196,8 +196,8 @@
 
     def body(
         rotor_ref, stator_ref, mortar_in, kf_in, kc_in, rf_in, rc_in,
-        rotor_out, stator_out, proj_out, back_out, wf_out, wc_out, rfs_out, rcs_out, df_out, dc_out,
-        mortar_ref, kf_ref, kc_ref, rf_ref, rc_ref, pad_ref, sem, small_sem,
+        rotor_out, stator_out, near1_out, near2_out, proj_out, back_out, proj_sum_out, back_sum_out,
+        wf_out, wc_out, rfs_out, rcs_out, df_out, dc_out, mortar_ref, kf_ref, kc_ref, rf_ref, rc_ref, pad_ref, sem, small_sem,
     ):
         copies = []
         for f in range(span):
@@ -222,7 +222,17 @@
         flipped = jnp.where(same, a_c * NF + a_r, -1)
         for c in little:
             c.wait()
-        for found, out in ((ahead, proj_out), (flipped, back_out)):
+
+        def both_terms(pair):
+            highs, lows = zip(*[parts_of(m) for m in pair])
+            return jnp.concatenate(
+                [jnp.concatenate([h, h], axis=1) for h in highs]
+                + [jnp.concatenate([l, jnp.zeros_like(l)], axis=1) for l in lows],
+                axis=0,
+            )
+
+        first_comp = (row < NF * NF) & (col < NF * NF)
+        for found, out, sum_out in ((ahead, proj_out, proj_sum_out), (flipped, back_out, back_sum_out)):
             pair = []
             for which in range(2):
                 total = jnp.zeros((tall, LANES), F32)
@@ -230,15 +240,9 @@
                 for i in range(NF):
                     for j in range(NF):
                         total = jnp.where(found == i * NF + j, matrix[i : i + 1, j : j + 1], total)
-                pair.append(total[:, :wide])
-            highs, lows = zip(*[parts_of(m) for m in pair])
-            out[...] = jnp.concatenate(
-                [
-                    jnp.concatenate([jnp.concatenate([h, h], axis=1) for h in highs], axis=0),
-                    jnp.concatenate([jnp.concatenate([l, jnp.zeros_like(l)], axis=1) for l in lows], axis=0),
-                ],
-                axis=0,
-            )
+                pair.append(total)
+            out[...] = both_terms([m[:, :wide] for m in pair])
+            sum_out[...] = both_terms([jnp.where(first_comp, m, 0.0)[:SUM_ROWS, :SUM_ROWS] for m in pair])
 
         def padded(ref, height, width):
             pad_ref[...] = jnp.zeros_like(pad_ref)
@@ -257,14 +261,21 @@
         rcs_out[...] = stacked(padded(rc_ref, 16, small))
         for c in copies:
             c.wait()
+        odd = lax.rem(lax.axis_index("sector"), 2) == 1
+        near1_out[0] = jnp.where(odd, rotor_out[0], rotor_out[span - 1])
+        near2_out[0] = jnp.where(odd, rotor_out[span - 1], rotor_out[0])
 
     return pl.pallas_call(
         body,
         out_shape=[
             jax.ShapeDtypeStruct((span, tall, LANES), F32),
             jax.ShapeDtypeStruct((span, tall, LANES), F32),
+            jax.ShapeDtypeStruct((1, tall, LANES), F32),
+            jax.ShapeDtypeStruct((1, tall, LANES), F32),
             jax.ShapeDtypeStruct((4 * tall, 2 * wide), BF16),
             jax.ShapeDtypeStruct((4 * tall, 2 * wide), BF16),
+            jax.ShapeDtypeStruct((4 * SUM_ROWS, 2 * SUM_ROWS), BF16),
+            jax.ShapeDtypeStruct((4 * SUM_ROWS, 2 * SUM_ROWS), BF16),
             jax.ShapeDtypeStruct((2 * big, 2 * big), BF16),
             jax.ShapeDtypeStruct((2 * small, 2 * small), BF16),
             jax.ShapeDtypeStruct((2 * small, 2 * big), BF16),
@@ -301,27 +312,21 @@
     lax.fori_loop(0, up(count, group) // group, some, 0, unroll=unroll)
 
 
-def own_part(rotor, near1, near2, proj, jac, diag):
+def own_part(rotor, proj, jac, diag):
     span, tall = rotor.shape[0], rotor.shape[1]
     wide = proj.shape[1] // 2
     e_total, height = jac.shape[0], diag.shape[0]
 
-    def body(r_in, near1_ref, near2_ref, proj_ref, jac_ref, diag_ref, kept, w_ref, y0, y1):
-        odd = lax.rem(lax.axis_index("sector"), 2) == 1
-        before = jnp.where(odd, near1_ref[0], near2_ref[0])
-        after = jnp.where(odd, near2_ref[0], near1_ref[0])
-
-        def rotor_slab(f):
-            inside = r_in[jnp.clip(f - 1, 0, span - 1)]
-            return jnp.where(f == 0, before, jnp.where(f == span + 1, after, inside))
-
-        apply_faces(proj_ref, rotor_slab, span + 2, tall, wide, y0, y1)
+    def body(r_in, proj_ref, jac_ref, diag_ref, kept, w_ref, y0, y1):
+        apply_faces(proj_ref, lambda f: r_in[f], span, tall, wide, y0, y1)
+        kept[0] = y0[0]
+        kept[span] = y1[span - 1]
 
         def face(g, carry):
-            kept[g] = y0[g + 1] + y1[g]
+            kept[g] = y0[g] + y1[g - 1]
             return carry
 
-        lax.fori_loop(0, span + 1, face, 0)
+        lax.fori_loop(1, span, face, 0)
         count = half_faces(NF, height)
 
         def weight(e, carry):
@@ -336,11 +341,11 @@
             jax.ShapeDtypeStruct((span + 1, tall, LANES), F32),
             jax.ShapeDtypeStruct((e_total, height, LANES), F32),
         ],
-        scratch_shapes=[pltpu.VMEM((up(span + 2, 4), tall, LANES), F32)] * 2,
+        scratch_shapes=[pltpu.VMEM((up(span, 4), tall, LANES), F32)] * 2,
         compiler_params=params(),
         cost_estimate=cost(2 * 10**9, 10 * 10**6),
         name="own_part",
-    )(rotor, near1, near2, proj, jac, diag)
+    )(rotor, proj, jac, diag)
 
 
 def join(far, near, near_s, far_s):
@@ -365,19 +370,95 @@
     )
 
 
-def first_sweep(shift, rotor_win, stator_win, stator, kept, proj, back, source, w, jac, weights, layers):
+def beside(near1_ref, near2_ref):
+    odd = lax.rem(lax.axis_index("sector"), 2) == 1
+    before = jnp.where(odd, near1_ref[0], near2_ref[0])
+    after = jnp.where(odd, near2_ref[0], near1_ref[0])
+    return before, after
+
+
+def stator_out(shift, rotor_win, stator, proj):
     span, tall = stator.shape[0], stator.shape[1]
-    wide = back.shape[1] // 2
+    wide = proj.shape[1] // 2
     rows = 4 * NF * NF
+
+    def body(shift_ref, rw_ref, s_in, proj_ref, out, y0, y1, flux, sem):
+        first = STEP - 1 - shift_ref[0]
+        apply_faces(proj_ref, lambda f: rw_ref[first + f], span + 1, tall, wide, y0, y1)
+        stores = []
+        for g in range(span):
+            flux[g] = s_in[g] - (y0[g + 1] + y1[g])
+            c = pltpu.make_async_copy(flux.at[g, pl.ds(0, rows), :], out.at[:, g, :], sem)
+            c.start()
+            stores.append(c)
+        for c in stores:
+            c.wait()
+
+    slabs = pltpu.VMEM((up(span + 1, 4), tall, LANES), F32)
+    return pl.pallas_call(
+        body,
+        out_shape=jax.ShapeDtypeStruct((rows, span, LANES), F32),
+        in_specs=[pl.BlockSpec(memory_space=pltpu.SMEM)] + [pl.BlockSpec()] * 3,
+        out_specs=hbm_spec(),
+        scratch_shapes=[slabs, slabs, pltpu.VMEM((span, tall, LANES), F32), pltpu.SemaphoreType.DMA],
+        compiler_params=params(),
+        cost_estimate=cost(10**9, 2 * 10**6),
+        name="stator_out",
+    )(shift, rotor_win, stator, proj)
+
+
+def rotor_out(shift, stator_win, kept, near1, near2, proj, back):
+    span, tall = kept.shape[0] - 1, kept.shape[1]
+    wide = proj.shape[1] // 2
+    rows = 4 * NF * NF
+
+    def body(shift_ref, sw_ref, kept_ref, near1_ref, near2_ref, proj_ref, back_ref, out, y0, y1, flux, sides, sem):
+        inner = shift_ref[0]
+        before, after = beside(near1_ref, near2_ref)
+        apply_faces(proj_ref, lambda f: jnp.where(f == 0, before, after), 2, tall, wide, y0, y1)
+        sides[0] = y1[0]
+        sides[1] = y0[1]
+
+        def jump(f):
+            own = kept_ref[f] + jnp.where(f == 0, sides[0], 0.0) + jnp.where(f == span, sides[1], 0.0)
+            return sw_ref[inner + f] - own
+
+        apply_faces(back_ref, jump, span + 1, tall, wide, y0, y1)
+        stores = []
+        for g in range(span):
+            flux[g] = y0[g] + y1[g + 1]
+            c = pltpu.make_async_copy(flux.at[g, pl.ds(0, rows), :], out.at[:, g, :], sem)
+            c.start()
+            stores.append(c)
+        for c in stores:
+            c.wait()
+
+    slabs = pltpu.VMEM((up(span + 1, 4), tall, LANES), F32)
+    return pl.pallas_call(
+        body,
+        out_shape=jax.ShapeDtypeStruct((rows, span, LANES), F32),
+        in_specs=[pl.BlockSpec(memory_space=pltpu.SMEM)] + [pl.BlockSpec()] * 6,
+        out_specs=hbm_spec(),
+        scratch_shapes=[
+            slabs, slabs, pltpu.VMEM((span, tall, LANES), F32), pltpu.VMEM((2, tall, LANES), F32), pltpu.SemaphoreType.DMA
+        ],
+        compiler_params=params(),
+        cost_estimate=cost(10**9, 2 * 10**6),
+        name="rotor_out",
+    )(shift, stator_win, kept, near1, near2, proj, back)
+
+
+def first_sweep(shift, rotor_win, stator_win, stator, kept, near1, near2, proj, back, source, w, jac, weights, layers):
+    span = stator.shape[0]
     e_total = jac.shape[0]
     n, nn = NF, NF * NF
     nodes = n**3
     height = weights.shape[0] // 2
+    group = 4
 
     def body(
-        shift_ref, rw_ref, sw_ref, s_in, kept_ref, proj_ref, back_ref, source_ref, w_ref, jac_ref, w_mat,
-        sflux_out, rflux_out, r_ref, u_ref, c1, c2, z1, z2,
-        y0, y1, x0, x1, sflux, rflux, count_ref, in_sem, out_sem,
+        shift_ref, rw_ref, sw_ref, s_in, kept_ref, near1_ref, near2_ref, proj_ref, back_ref, source_ref, w_ref,
+        jac_ref, w_mat, r_ref, u_ref, c1, c2, z1, z2, x, y0, y1, count_ref, in_sem,
     ):
         loads = [
             pltpu.make_async_copy(source_ref.at[:, e, :], r_ref.at[e, pl.ds(0, nodes), :], in_sem)
@@ -388,54 +469,63 @@
         inner = shift_ref[0]
         first_rotor = STEP - 1 - inner
         count_ref[...] = half_faces(n, height)
-        apply_faces(proj_ref, lambda f: rw_ref[first_rotor + f], span + 1, tall, wide, x0, x1, unroll=FACE_UNROLL)
-        apply_faces(
-            back_ref, lambda f: sw_ref[inner + f] - kept_ref[f], span + 1, tall, wide, y0, y1, unroll=FACE_UNROLL
-        )
-        stores = []
-        for s in range(span):
-            sflux[s] = s_in[s] - (x0[s + 1] + x1[s])
-            rflux[s] = y0[s] + y1[s + 1]
-            for buffer, out in ((sflux, sflux_out), (rflux, rflux_out)):
-                c = pltpu.make_async_copy(buffer.at[s, pl.ds(0, rows), :], out.at[:, s, :], out_sem)
-                c.start()
-                stores.append(c)
+
+        def summed(slab):
+            return slab[:nn] + slab[3 * nn : 4 * nn]
+
+        def sum_of(ref, f):
+            return ref[f, pl.ds(0, nn), :] + ref[f, pl.ds(3 * nn, nn), :]
+
+        def apply(matrix_ref, count):
+            for i in range(0, count, group):
+                high, low = parts_of(jnp.concatenate([x[i + j] for j in range(group)], axis=1))
+                y = jnp.dot(matrix_ref[...], jnp.concatenate([high, low], axis=0), preferred_element_type=F32)
+                a = y[:SUM_ROWS] + y[2 * SUM_ROWS : 3 * SUM_ROWS]
+                b = y[SUM_ROWS : 2 * SUM_ROWS] + y[3 * SUM_ROWS :]
+                for j in range(group):
+                    y0[i + j] = a[:, j * LANES : (j + 1) * LANES]
+                    y1[i + j] = b[:, j * LANES : (j + 1) * LANES]
+
+        x[...] = jnp.zeros_like(x)
+        for f in range(span + 1):
+            x[f, pl.ds(0, nn), :] = sum_of(rw_ref, first_rotor + f)
+        before, after = beside(near1_ref, near2_ref)
+        x[span + 1, pl.ds(0, nn), :] = summed(before)
+        x[span + 2, pl.ds(0, nn), :] = summed(after)
+        apply(proj_ref, up(span + 3, group))
+        inflow = [sum_of(s_in, g) - (y0[g + 1] + y1[g])[:nn] for g in range(span)]
         for c in loads:
             c.wait()
         for s in range(span):
             if height > nodes:
                 for layer in range(layers):
                     r_ref[layer * span + s, pl.ds(nodes, height - nodes), :] = jnp.zeros((height - nodes, LANES), F32)
-            inflow = sflux[s, pl.ds(0, nn), :] + sflux[s, pl.ds(3 * nn, nn), :]
-            outflow = rflux[s, pl.ds(0, nn), :] + rflux[s, pl.ds(3 * nn, nn), :]
-            r_ref[span + s, pl.ds(0, nn, stride=n), :] += inflow
-            r_ref[s, pl.ds(n - 1, nn, stride=n), :] += -outflow
+            r_ref[span + s, pl.ds(0, nn, stride=n), :] += inflow[s]
+        for f in range(span + 1):
+            own = sum_of(kept_ref, f)
+            if f == 0:
+                own = own + y1[span + 1, pl.ds(0, nn), :]
+            if f == span:
+                own = own + y0[span + 2, pl.ds(0, nn), :]
+            x[f, pl.ds(0, nn), :] = sum_of(sw_ref, inner + f) - own
+        apply(back_ref, up(span + 1, group))
+        for s in range(span):
+            r_ref[s, pl.ds(n - 1, nn, stride=n), :] += -(y0[s] + y1[s + 1])[:nn]
         correct(n, e_total, span, r_ref, u_ref, lambda e, r: r * w_ref[e], c1, c2, z1, z2)
         subtract_operator(n, e_total, span, r_ref, u_ref, w_mat, jac_ref, count_ref)
-        for c in stores:
-            c.wait()
 
     whole = pl.BlockSpec()
     field = jax.ShapeDtypeStruct((e_total, height, LANES), F32)
-    trace = jax.ShapeDtypeStruct((rows, span, LANES), F32)
-    slabs = pltpu.VMEM((up(span + 1, 4), tall, LANES), F32)
+    slabs = pltpu.VMEM((up(span + 3, group), SUM_ROWS, LANES), F32)
     return pl.pallas_call(
         body,
-        out_shape=[trace, trace, field, field] + face_shapes(n, layers),
-        in_specs=[pl.BlockSpec(memory_space=pltpu.SMEM)] + [whole] * 6 + [hbm_spec()] + [whole] * 3,
-        out_specs=[hbm_spec()] * 2 + [whole] * 6,
-        scratch_shapes=[slabs] * 4
-        + [
-            pltpu.VMEM((span, tall, LANES), F32),
-            pltpu.VMEM((span, tall, LANES), F32),
-            pltpu.VMEM((height, LANES), F32),
-            pltpu.SemaphoreType.DMA,
-            pltpu.SemaphoreType.DMA,
-        ],
+        out_shape=[field, field] + face_shapes(n, layers),
+        in_specs=[pl.BlockSpec(memory_space=pltpu.SMEM)] + [whole] * 8 + [hbm_spec()] + [whole] * 3,
+        scratch_shapes=[slabs] * 3 + [pltpu.VMEM((height, LANES), F32), pltpu.SemaphoreType.DMA],
         compiler_params=params(),
         cost_estimate=cost(2 * 10**9, 20 * 10**6),
         name="first_sweep",
-    )(shift, rotor_win, stator_win, stator, kept, proj, back, *in_hbm(source), w, jac, weights)
+    )(shift, rotor_win, stator_win, stator, kept, near1, near2, proj, back, *in_hbm(source), w, jac, weights)
 
 
 def sweep(n, r, p, w, jac, weights, faces, layers, last):
@@ -602,7 +692,7 @@
     span = rotor.shape[0]
     sectors = lax.axis_size("sector")
     buckets = span // STEP
-    device, rest = offset // span, offset % span
+    device, rest = lax.div(offset, span), lax.rem(offset, span)
 
     def branch(number):
         by, bucket = number // buckets, number % buckets
@@ -618,8 +708,8 @@
 
         return run
 
-    choice = device * buckets + rest // STEP
-    shift = (rest % STEP).reshape(1)
+    choice = device * buckets + lax.div(rest, STEP)
+    shift = lax.rem(rest, STEP).reshape(1)
     return shift, lax.switch(choice, [branch(i) for i in range(sectors * buckets)], rotor, stator, own)
 
 
@@ -633,18 +723,17 @@
     jac = jacobian.reshape(e_total, axial)
     rotor_rows = rotor_trace.reshape(-1, span, axial)
     stator_rows = stator_trace.reshape(-1, span, axial)
-    rotor, stator, proj, back, wf, wc, rfs, rcs, df, dc = prepare(
+    rotor, stator, near1, near2, proj, back, proj_sum, back_sum, wf, wc, rfs, rcs, df, dc = prepare(
         rotor_rows, stator_rows, mortar_proj.transpose(1, 0, 2), stiff_fine, stiff_coarse, restrict_fine, restrict_coarse
     )
-    odd = lax.axis_index("sector") % 2 == 1
-    first, final = rotor[:1], rotor[span - 1 :]
-    near1 = swap(jnp.where(odd, first, final), "sector", False)
-    near2 = swap(jnp.where(odd, final, first), "sector", True)
-    own = (near1, near2, proj, jac, df)
-    shift, (rotor_win, stator_win, kept, w) = windows(rotor, stator, offsets[0], own)
-    sflux, rflux, r, p, *faces = first_sweep(
-        shift, rotor_win, stator_win, stator, kept, proj, back, source_rows, w, jac, wf, layers
+    near2 = swap(near2, "sector", True)
+    near1 = swap(near1, "sector", False)
+    shift, (rotor_win, stator_win, kept, w) = windows(rotor, stator, offsets[0], (proj, jac, df))
+    r, p, *faces = first_sweep(
+        shift, rotor_win, stator_win, stator, kept, near1, near2, proj_sum, back_sum, source_rows, w, jac, wf, layers
     )
+    sflux = stator_out(shift, rotor_win, stator, proj)
+    rflux = rotor_out(shift, stator_win, kept, near1, near2, proj, back)
     p, r, *faces = sweep(NF, r, p, w, jac, wf, exchange(faces), layers, False)
     fine, r, *faces = sweep(NF, r, p, w, jac, wf, exchange(faces), layers, True)
     r, p, w, *faces = to_coarse(r, exchange(faces), rfs, jac, wc, dc, layers)

time: 106 us -> 107 us (level)
  waiting for transfers between devices: 21.8 us -> 17.2 us
  Pallas kernels: 26.2 us -> 29.4 us
  starting transfers between devices: 54.9 us -> 58 us
    ppermute x20, waiting for transfers between devices: 18.4 us -> 12 us  [swap(): return lax.ppermute(x, axis, pairs)]
    pallas_call x1 -> x3, Pallas kernels: 7.5 us -> 11.1 us  [the longest x1 6.12 us: first_sweep(): pl.pallas_call(body, out_shape=[field, field] + face_shapes(n, layers), i...]
    ppermute x20, starting transfers between devices: 52 us -> 54.2 us  [swap(): return lax.ppermute(x, axis, pairs)]
    ppermute x4, waiting for transfers between devices: 3.4 us -> 5.22 us  [move(): return lax.ppermute(x, axis, [(i, (i + by) % count) for i in range(count)])]
    pallas_call x1, Pallas kernels: 4.84 us -> 3.26 us  [own_part(): pl.pallas_call(body, out_shape=[jax.ShapeDtypeStruct((span + 1, tall, LAN...]
  transfers between devices with their start and end apart: 30 -> 30, of which waited for: 12 -> 9; matrix products, arithmetic and copies ran while one was open for 0% -> 0% of each run, Pallas kernels for 5% -> 9%
where the time goes in v1:
time: 107 us
  starting transfers between devices  58 us (54%)
  Pallas kernels  29.4 us (27%)
  waiting for transfers between devices  17.2 us (16%)
  between operations  1.68 us (2%)
    ppermute x20, starting transfers between devices, swap(): return lax.ppermute(x, axis, pairs)  54.2 us
    ppermute x20, waiting for transfers between devices, swap(): return lax.ppermute(x, axis, pairs)  12 us
    pallas_call x4, Pallas kernels, sweep(): pl.pallas_call(body, out_shape=[kept, field] + face_shapes(n, layers), ou...  7.37 us
    pallas_call x1, Pallas kernels, first_sweep(): pl.pallas_call(body, out_shape=[field, field] + face_shapes(n, layers), i...  6.12 us
    ppermute x4, waiting for transfers between devices, move(): return lax.ppermute(x, axis, [(i, (i + by) % count) for i in range(count)])  5.22 us
    ppermute x4, starting transfers between devices, move(): return lax.ppermute(x, axis, [(i, (i + by) % count) for i in range(count)])  3.75 us
    pallas_call x1, Pallas kernels, own_part(): pl.pallas_call(body, out_shape=[jax.ShapeDtypeStruct((span + 1, tall, LAN...  3.26 us
    pallas_call x1, Pallas kernels, prepare(): pl.pallas_call(body, out_shape=[jax.ShapeDtypeStruct((span, tall, LANES),...  2.96 us
  transfers between devices with their start and end apart: 30, of which 9 were waited for; matrix products, arithmetic and copies ran while one was open for 0% of the time, Pallas kernels for 9%

profile of v1, /device:TPU:0, one launch (start us, length us, event | category | flops | bytes accessed | tf_op | source)
XLA Modules:
  0.0 106.5 jit_solution(5385155041696400439)
XLA Ops:
  0.6 3.0 %prepare.1 = (f32[16,104,128]{2,1,0:T(8,128)S(1)}, f32[16,104,128]{2,1,0:T(8,128)S(1)}, f32[1,104,128]{2,1,0:T(8,128)S(1)}, f32[1,104,128]{2,1,0:T(8,128)S(1)}, ...) custom-call(f32[100,16,128]{2,1,0:T(8,128)} %bitcast.16, ...), custom_call_target="tpu_custom_call" | custom-call | tf_op jit(solution)/shard_map/prepare/pallas_call | solution.py:268
  3.6 0.6 collective-permute-start.128
  4.9 13.7 %conditional.1 = (f32[20,104,128]{2,1,0:T(8,128)S(1)}, f32[20,104,128]{2,1,0:T(8,128)}, f32[17,104,128]{2,1,0:T(8,128)S(1)}, f32[32,128,128]{2,1,0:T(8,128)}) conditional(s32[]{:T(128)} %clamp.3, (f32[16,104,128]{2,1,0:T(8,128)S(1)}, f32[16,104,128]{2,1,0:T(8,128)S(1)}, bf16[416,224]{1,0:T(8,128)(2,1)}, ...), branch_computations={%region_0.0_spmd, %region_1.0_spmd, %region_2.0_spmd, %region_3.0_... | conditional | flops 2000000000 | bytes 23525212 | solution.py:713
  4.9 0.0 collective-permute-start.5
  5.0 0.0 copy-start.4
  5.1 0.0 collective-permute-start.6
  5.1 0.1 collective-permute-start.4
  5.2 3.6 %collective-permute-start.7 = (f32[8,104,128]{2,1,0:T(8,128)S(1)}, f32[8,104,128]{2,1,0:T(8,128)S(1)}, u32[]{:S(2)}, u32[]{:S(2)}) collective-permute-start(f32[8,104,128]{2,1,0:T(8,128)S(1)} %slice.197), channel_id=1, source_target_pairs={{0,28},{4,0},{8,4},{12,8},{16,12},{20,16},{24,20},{28,24},{1,29},{... | collective-permute-start | bytes 1277960 | tf_op jit(solution)/shard_map/cond/branch_1_fun/ppermute | solution.py:659
  8.8 3.3 %own_part.33 = (f32[17,104,128]{2,1,0:T(8,128)S(1)}, f32[32,128,128]{2,1,0:T(8,128)}) custom-call(f32[16,104,128]{2,1,0:T(8,128)S(1)} %get-tuple-element.329.r_in, bf16[416,224]{1,0:T(8,128)(2,1)S(1)} %copy-done.4, f32[32,128]{1,0:T(8,128)S(1)} %get-tuple-element.334.jac_ref, f32[128,128]{1,0:T(8,128)S(1)} %get-tuple-element.335.diag_ref), custom_call_target="tpu_custom_call" | custom-call | flops 2000000000 | bytes 10000000 | tf_op jit(solution)/shard_map/cond/branch_1_fun/own_part/pallas_call | solution.py:338
  12.1 5.0 %collective-permute-done.4.far_ref = f32[8,104,128]{2,1,0:T(8,128)S(1)} collective-permute-done((f32[8,104,128]{2,1,0:T(8,128)S(1)}, f32[8,104,128]{2,1,0:T(8,128)S(1)}, u32[]{:S(2)}, u32[]{:S(2)}) %collective-permute-start.4) | collective-permute-done | bytes 426016 | tf_op jit(solution)/shard_map/cond/branch_1_fun/ppermute | solution.py:659
  17.1 0.2 collective-permute-done.7.far_s_ref
  17.3 1.2 %join.33 = (f32[20,104,128]{2,1,0:T(8,128)S(1)}, f32[20,104,128]{2,1,0:T(8,128)}) custom-call(f32[8,104,128]{2,1,0:T(8,128)S(1)} %collective-permute-done.4.far_ref, f32[12,104,128]{2,1,0:T(8,128)S(1)} %collective-permute-done.5.near_ref, f32[12,104,128]{2,1,0:T(8,128)S(1)} %collective-permute-done.6.near_s_ref, ...), custom_call_target="tpu_custom_call" | custom-call | tf_op jit(solution)/shard_map/cond/branch_1_fun/join/pallas_call | solution.py:368
  18.5 2.8 %collective-permute-start.129 = (f32[1,104,128]{2,1,0:T(8,128)S(1)}, f32[1,104,128]{2,1,0:T(8,128)S(1)}, u32[]{:S(2)}, u32[]{:S(2)}) collective-permute-start(f32[1,104,128]{2,1,0:T(8,128)S(1)} %get-tuple-element.676), channel_id=1, source_target_pairs={{0,28},{4,8},{8,4},{12,16},{16,12},{20,24},{24,20},{28,0},{1,29},{... | collective-permute-start | bytes 159752 | tf_op jit(solution)/shard_map/ppermute | solution.py:668
  21.3 1.8 %collective-permute-done.129.near2_ref = f32[1,104,128]{2,1,0:T(8,128)S(1)} collective-permute-done((f32[1,104,128]{2,1,0:T(8,128)S(1)}, f32[1,104,128]{2,1,0:T(8,128)S(1)}, u32[]{:S(2)}, u32[]{:S(2)}) %collective-permute-start.129) | collective-permute-done | bytes 53280 | tf_op jit(solution)/shard_map/ppermute | solution.py:668
  23.2 6.1 %first_sweep.1 = (f32[32,128,128]{2,1,0:T(8,128)S(1)}, f32[32,128,128]{2,1,0:T(8,128)S(1)}, f32[2,25,128]{2,1,0:T(8,128)S(1)}, f32[2,25,128]{2,1,0:T(8,128)S(1)}...) custom-call(s32[1]{0:T(128)} %bitcast.1.shift_ref, f32[20,104,128]{2,1,0:T(8,128)S(1)} %get-tuple-element.672.rw_ref, ...), custom_call_target="tpu_custom_call" | custom-call | flops 2000000000 | bytes 20000000 | tf_op jit(solution)/shard_map/first_sweep/pallas_call | solution.py:520
  29.3 1.3 %collective-permute-start.130 = (f32[2,25,128]{2,1,0:T(8,128)S(1)}, f32[2,25,128]{2,1,0:T(8,128)S(1)}, u32[]{:S(2)}, u32[]{:S(2)}) collective-permute-start(f32[2,25,128]{2,1,0:T(8,128)S(1)} %get-tuple-element.684), channel_id=1, source_target_pairs={{0,4},{4,0},{8,12},{12,8},{16,20},{20,16},{24,28},{28,24},{1,5},{5... | collective-permute-start | bytes 76808 | tf_op jit(solution)/shard_map/ppermute | solution.py:668
  30.6 1.4 %collective-permute-start.131 = (f32[2,25,128]{2,1,0:T(8,128)S(1)}, f32[2,25,128]{2,1,0:T(8,128)S(1)}, u32[]{:S(2)}, u32[]{:S(2)}) collective-permute-start(f32[2,25,128]{2,1,0:T(8,128)S(1)} %get-tuple-element.685), channel_id=1, source_target_pairs={{0,28},{4,8},{8,4},{12,16},{16,12},{20,24},{24,20},{28,0},{1,29},{... | collective-permute-start | bytes 76808 | tf_op jit(solution)/shard_map/ppermute | solution.py:668
  32.1 33.8 %collective-permute-start.132 = (f32[5,8,128]{2,1,0:T(8,128)S(1)}, f32[5,8,128]{2,1,0:T(8,128)S(1)}, u32[]{:S(2)}, u32[]{:S(2)}) collective-permute-start(f32[5,8,128]{2,1,0:T(8,128)S(1)} %get-tuple-element.686), channel_id=1, source_target_pairs={{0,1},{1,0},{2,3},{3,2},{4,5},{5,4},{6,7},{7,6},{8,9},{9,8},{10,11... | collective-permute-start | bytes 61448 | tf_op jit(solution)/shard_map/ppermute | solution.py:668
  65.8 1.8 %collective-permute-done.132.g1 = f32[5,8,128]{2,1,0:T(8,128)S(1)} collective-permute-done((f32[5,8,128]{2,1,0:T(8,128)S(1)}, f32[5,8,128]{2,1,0:T(8,128)S(1)}, u32[]{:S(2)}, u32[]{:S(2)}) %collective-permute-start.132) | collective-permute-done | bytes 20512 | tf_op jit(solution)/shard_map/ppermute | solution.py:668
  67.6 2.5 %shard_map.137 = (f32[32,128,128]{2,1,0:T(8,128)S(1)}, f32[32,128,128]{2,1,0:T(8,128)S(1)}, f32[2,25,128]{2,1,0:T(8,128)S(1)}, f32[2,25,128]{2,1,0:T(8,128)S(1)}...) custom-call(f32[32,128,128]{2,1,0:T(8,128)S(1)} %get-tuple-element.682.r_in, ...), custom_call_target="tpu_custom_call" | custom-call | flops 1000000000 | bytes 10000000 | tf_op jit(solution)/shard_map/pallas_call | solution.py:560
  70.1 0.1 collective-permute-start.134
  70.2 0.8 collective-permute-start.135
  70.9 2.2 %collective-permute-start.136 = (f32[5,8,128]{2,1,0:T(8,128)S(1)}, f32[5,8,128]{2,1,0:T(8,128)S(1)}, u32[]{:S(2)}, u32[]{:S(2)}) collective-permute-start(f32[5,8,128]{2,1,0:T(8,128)S(1)} %get-tuple-element.692), channel_id=1, source_target_pairs={{0,1},{1,0},{2,3},{3,2},{4,5},{5,4},{6,7},{7,6},{8,9},{9,8},{10,11... | collective-permute-start | bytes 61448 | tf_op jit(solution)/shard_map/ppermute | solution.py:668
  73.1 1.8 %collective-permute-done.136.g1 = f32[5,8,128]{2,1,0:T(8,128)S(1)} collective-permute-done((f32[5,8,128]{2,1,0:T(8,128)S(1)}, f32[5,8,128]{2,1,0:T(8,128)S(1)}, u32[]{:S(2)}, u32[]{:S(2)}) %collective-permute-start.136) | collective-permute-done | bytes 20512 | tf_op jit(solution)/shard_map/ppermute | solution.py:668
  74.9 2.5 %shard_map.138 = (f32[125,32,128]{2,1,0:T(8,128)}, f32[32,128,128]{2,1,0:T(8,128)S(1)}, f32[2,25,128]{2,1,0:T(8,128)S(1)}, f32[2,25,128]{2,1,0:T(8,128)S(1)}, f3...) custom-call(f32[32,128,128]{2,1,0:T(8,128)S(1)} %get-tuple-element.688.r_in, ...), custom_call_target="tpu_custom_call" | custom-call | flops 1000000000 | bytes 10000000 | tf_op jit(solution)/shard_map/pallas_call | solution.py:560
  77.4 0.1 collective-permute-start.138
  77.5 1.5 %collective-permute-start.139 = (f32[2,25,128]{2,1,0:T(8,128)S(1)}, f32[2,25,128]{2,1,0:T(8,128)S(1)}, u32[]{:S(2)}, u32[]{:S(2)}) collective-permute-start(f32[2,25,128]{2,1,0:T(8,128)S(1)} %get-tuple-element.697), channel_id=1, source_target_pairs={{0,28},{4,8},{8,4},{12,16},{16,12},{20,24},{24,20},{28,0},{1,29},{... | collective-permute-start | bytes 76808 | tf_op jit(solution)/shard_map/ppermute | solution.py:668
  79.0 2.0 %collective-permute-start.140 = (f32[5,8,128]{2,1,0:T(8,128)S(1)}, f32[5,8,128]{2,1,0:T(8,128)S(1)}, u32[]{:S(2)}, u32[]{:S(2)}) collective-permute-start(f32[5,8,128]{2,1,0:T(8,128)S(1)} %get-tuple-element.698), channel_id=1, source_target_pairs={{0,1},{1,0},{2,3},{3,2},{4,5},{5,4},{6,7},{7,6},{8,9},{9,8},{10,11... | collective-permute-start | bytes 61448 | tf_op jit(solution)/shard_map/ppermute | solution.py:668
  81.0 1.8 %collective-permute-done.140.g1 = f32[5,8,128]{2,1,0:T(8,128)S(1)} collective-permute-done((f32[5,8,128]{2,1,0:T(8,128)S(1)}, f32[5,8,128]{2,1,0:T(8,128)S(1)}, u32[]{:S(2)}, u32[]{:S(2)}) %collective-permute-start.140) | collective-permute-done | bytes 20512 | tf_op jit(solution)/shard_map/ppermute | solution.py:668
  82.8 2.2 %to_coarse.1 = (f32[32,32,128]{2,1,0:T(8,128)S(1)}, f32[32,32,128]{2,1,0:T(8,128)S(1)}, f32[32,32,128]{2,1,0:T(8,128)S(1)}, f32[2,9,128]{2,1,0:T(8,128)S(1)}, f3...) custom-call(f32[32,128,128]{2,1,0:T(8,128)S(1)} %get-tuple-element.695.r_in, ...), custom_call_target="tpu_custom_call" | custom-call | flops 500000000 | bytes 5000000 | tf_op jit(solution)/shard_map/to_coarse/pallas_call | solution.py:605
  85.1 2.1 %collective-permute-start.144 = (f32[3,8,128]{2,1,0:T(8,128)S(1)}, f32[3,8,128]{2,1,0:T(8,128)S(1)}, u32[]{:S(2)}, u32[]{:S(2)}) collective-permute-start(f32[3,8,128]{2,1,0:T(8,128)S(1)} %get-tuple-element.708), channel_id=1, source_target_pairs={{0,1},{1,0},{2,3},{3,2},{4,5},{5,4},{6,7},{7,6},{8,9},{9,8},{10,11... | collective-permute-start | bytes 36872 | tf_op jit(solution)/shard_map/ppermute | solution.py:668
  87.1 0.5 collective-permute-start.142
  87.6 1.0 collective-permute-start.143
  88.7 3.2 %collective-permute-done.143.h2 = f32[2,9,128]{2,1,0:T(8,128)S(1)} collective-permute-done((f32[2,9,128]{2,1,0:T(8,128)S(1)}, f32[2,9,128]{2,1,0:T(8,128)S(1)}, u32[]{:S(2)}, u32[]{:S(2)}) %collective-permute-start.143) | collective-permute-done | bytes 9248 | tf_op jit(solution)/shard_map/ppermute | solution.py:668
  91.9 1.2 %shard_map.139 = (f32[32,32,128]{2,1,0:T(8,128)S(1)}, f32[32,32,128]{2,1,0:T(8,128)S(1)}, f32[2,9,128]{2,1,0:T(8,128)S(1)}, f32[2,9,128]{2,1,0:T(8,128)S(1)}, f3...) custom-call(f32[32,32,128]{2,1,0:T(8,128)S(1)} %get-tuple-element.703.r_in, f32[32,32,128]{2,1,0:T(8,128)S(1)} %get-tuple-element.704.p_in, ...), custom_call_target="tpu_custom_call" | custom-call | flops 100000000 | bytes 10000000 | tf_op jit(solution)/shard_map/pallas_call | solution.py:560
  93.0 0.1 collective-permute-start.148
  93.1 0.1 collective-permute-start.149
  93.2 0.5 collective-permute-start.146
  93.7 0.9 collective-permute-start.147
  94.6 2.3 %stator_out.1 = f32[100,16,128]{2,1,0:T(8,128)} custom-call(s32[1]{0:T(128)} %bitcast.1.shift_ref, f32[20,104,128]{2,1,0:T(8,128)S(1)} %get-tuple-element.672.rw_ref, f32[16,104,128]{2,1,0:T(8,128)S(1)} %get-tuple-element.669.s_in, bf16[416,224]{1,0:T(8,128)(2,1)S(1)} %copy-done.3), custom_call_target="tpu_custom_call" | custom-call | flops 1000000000 | bytes 2000000 | tf_op jit(solution)/shard_map/stator_out/pallas_call | solution.py:398
  96.9 1.0 collective-permute-done.147.h2
  97.8 1.2 %shard_map.140 = (f32[27,32,128]{2,1,0:T(8,128)}, f32[32,32,128]{2,1,0:T(8,128)S(1)}, f32[2,9,128]{2,1,0:T(8,128)S(1)}, f32[2,9,128]{2,1,0:T(8,128)S(1)}, f32[3,...) custom-call(f32[32,32,128]{2,1,0:T(8,128)S(1)} %get-tuple-element.710.r_in, f32[32,32,128]{2,1,0:T(8,128)S(1)} %get-tuple-element.711.p_in, ...), custom_call_target="tpu_custom_call" | custom-call | flops 100000000 | bytes 10000000 | tf_op jit(solution)/shard_map/pallas_call | solution.py:560
  99.1 1.4 %collective-permute-start.152 = (f32[3,8,128]{2,1,0:T(8,128)S(1)}, f32[3,8,128]{2,1,0:T(8,128)S(1)}, u32[]{:S(2)}, u32[]{:S(2)}) collective-permute-start(f32[3,8,128]{2,1,0:T(8,128)S(1)} %get-tuple-element.720), channel_id=1, source_target_pairs={{0,1},{1,0},{2,3},{3,2},{4,5},{5,4},{6,7},{7,6},{8,9},{9,8},{10,11... | collective-permute-start | bytes 36872 | tf_op jit(solution)/shard_map/ppermute | solution.py:668
  100.5 0.5 collective-permute-start.150
  101.0 0.6 collective-permute-start.151
  101.6 2.7 %rotor_out.1 = f32[100,16,128]{2,1,0:T(8,128)} custom-call(s32[1]{0:T(128)} %bitcast.1.shift_ref, f32[20,104,128]{2,1,0:T(8,128)S(1)} %copy-done.1, f32[17,104,128]{2,1,0:T(8,128)S(1)} %get-tuple-element.674.kept_ref, f32[1,104,128]{2,1,0:T(8,128)S(1)} %collective-permute-done.128.near1_ref, f32[1,104,128]{2,1,0:T(8,128)S(1)} %collective-permute-done.129.near2_ref, ...), custom_call_target="tpu_custom_call" | custom-call | flops 1000000000 | bytes 2000000 | tf_op jit(solution)/shard_map/rotor_out/pallas_call | solution.py:437
  104.4 0.7 collective-permute-done.151.h2
  105.1 1.2 %to_coarsest.1 = f32[8,32,128]{2,1,0:T(8,128)} custom-call(f32[32,32,128]{2,1,0:T(8,128)S(1)} %get-tuple-element.717.r_in, f32[2,9,128]{2,1,0:T(8,128)S(1)} %collective-permute-done.150.h1, f32[2,9,128]{2,1,0:T(8,128)S(1)} %collective-permute-done.151.h2, f32[3,8,128]{2,1,0:T(8,128)S(1)} %collective-permute-done.152.g1, ...), custom_call_target="tpu_custom_call" | custom-call | flops 50000000 | bytes 1000000 | tf_op jit(solution)/shard_map/to_coarsest/pallas_call | solution.py:641
  (39 shorter events, 0.2 us)
Async XLA Ops:
  0.6 4.2 %copy-start.2 = (f32[2,16,128]{2,1,0:T(8,128)S(1)}, f32[2,16,128]{2,1,0:T(8,128)}, u32[]{:S(2)}) copy-start(f32[2,16,128]{2,1,0:T(8,128)} %param.43) | copy-start | bytes 49156
  3.6 17.7 %collective-permute-start.128 = (f32[1,104,128]{2,1,0:T(8,128)S(1)}, f32[1,104,128]{2,1,0:T(8,128)S(1)}, u32[]{:S(2)}, u32[]{:S(2)}) collective-permute-start(f32[1,104,128]{2,1,0:T(8,128)S(1)} %get-tuple-element.675), channel_id=1, source_target_pairs={{0,4},{4,0},{8,12},{12,8},{16,20},{20,16},{24,28},{28,24},{1,5},{5... | collective-permute-start | bytes 159752 | tf_op jit(solution)/shard_map/ppermute | solution.py:668
  4.9 12.4 %collective-permute-start.5 = (f32[12,104,128]{2,1,0:T(8,128)S(1)}, f32[12,104,128]{2,1,0:T(8,128)S(1)}, u32[]{:S(2)}, u32[]{:S(2)}) collective-permute-start(f32[12,104,128]{2,1,0:T(8,128)S(1)} %slice.195), channel_id=1, source_target_pairs={{0,0},{4,4},{8,8},{12,12},{16,16},{20,20},{24,24},{28,28},{1,1},{5... | collective-permute-start | bytes 1916936 | tf_op jit(solution)/shard_map/cond/branch_1_fun/ppermute | solution.py:659
  5.0 3.8 %copy-start.4 = (bf16[416,224]{1,0:T(8,128)(2,1)S(1)}, bf16[416,224]{1,0:T(8,128)(2,1)}, u32[]{:S(2)}) copy-start(bf16[416,224]{1,0:T(8,128)(2,1)} %get-tuple-element.333.proj_ref) | copy-start | bytes 559108 | tf_op jit(solution)/shard_map/cond
  5.1 12.3 %collective-permute-start.6 = (f32[12,104,128]{2,1,0:T(8,128)S(1)}, f32[12,104,128]{2,1,0:T(8,128)S(1)}, u32[]{:S(2)}, u32[]{:S(2)}) collective-permute-start(f32[12,104,128]{2,1,0:T(8,128)S(1)} %slice.196), channel_id=1, source_target_pairs={{0,0},{4,4},{8,8},{12,12},{16,16},{20,20},{24,24},{28,28},{1,1},{5... | collective-permute-start | bytes 1916936 | tf_op jit(solution)/shard_map/cond/branch_1_fun/ppermute | solution.py:659
  5.1 12.0 %collective-permute-start.4 = (f32[8,104,128]{2,1,0:T(8,128)S(1)}, f32[8,104,128]{2,1,0:T(8,128)S(1)}, u32[]{:S(2)}, u32[]{:S(2)}) collective-permute-start(f32[8,104,128]{2,1,0:T(8,128)S(1)} %slice.194), channel_id=1, source_target_pairs={{0,4},{4,8},{8,12},{12,16},{16,20},{20,24},{24,28},{28,0},{1,5},{5... | collective-permute-start | bytes 1277960 | tf_op jit(solution)/shard_map/cond/branch_1_fun/ppermute | solution.py:659
  5.2 12.1 %collective-permute-start.7 = (f32[8,104,128]{2,1,0:T(8,128)S(1)}, f32[8,104,128]{2,1,0:T(8,128)S(1)}, u32[]{:S(2)}, u32[]{:S(2)}) collective-permute-start(f32[8,104,128]{2,1,0:T(8,128)S(1)} %slice.197), channel_id=1, source_target_pairs={{0,28},{4,0},{8,4},{12,8},{16,12},{20,16},{24,20},{28,24},{1,29},{... | collective-permute-start | bytes 1277960 | tf_op jit(solution)/shard_map/cond/branch_1_fun/ppermute | solution.py:659
  18.5 4.6 %collective-permute-start.129 = (f32[1,104,128]{2,1,0:T(8,128)S(1)}, f32[1,104,128]{2,1,0:T(8,128)S(1)}, u32[]{:S(2)}, u32[]{:S(2)}) collective-permute-start(f32[1,104,128]{2,1,0:T(8,128)S(1)} %get-tuple-element.676), channel_id=1, source_target_pairs={{0,28},{4,8},{8,4},{12,16},{16,12},{20,24},{24,20},{28,0},{1,29},{... | collective-permute-start | bytes 159752 | tf_op jit(solution)/shard_map/ppermute | solution.py:668
  23.2 44.4 %copy-start = (f32[32,128,128]{2,1,0:T(8,128)S(1)}, f32[32,128,128]{2,1,0:T(8,128)}, u32[]{:S(2)}) copy-start(f32[32,128,128]{2,1,0:T(8,128)} %get-tuple-element.680.w_ref.w_in) | copy-start | bytes 6291460
  29.3 38.3 %collective-permute-start.130 = (f32[2,25,128]{2,1,0:T(8,128)S(1)}, f32[2,25,128]{2,1,0:T(8,128)S(1)}, u32[]{:S(2)}, u32[]{:S(2)}) collective-permute-start(f32[2,25,128]{2,1,0:T(8,128)S(1)} %get-tuple-element.684), channel_id=1, source_target_pairs={{0,4},{4,0},{8,12},{12,8},{16,20},{20,16},{24,28},{28,24},{1,5},{5... | collective-permute-start | bytes 76808 | tf_op jit(solution)/shard_map/ppermute | solution.py:668
  30.6 37.0 %collective-permute-start.131 = (f32[2,25,128]{2,1,0:T(8,128)S(1)}, f32[2,25,128]{2,1,0:T(8,128)S(1)}, u32[]{:S(2)}, u32[]{:S(2)}) collective-permute-start(f32[2,25,128]{2,1,0:T(8,128)S(1)} %get-tuple-element.685), channel_id=1, source_target_pairs={{0,28},{4,8},{8,4},{12,16},{16,12},{20,24},{24,20},{28,0},{1,29},{... | collective-permute-start | bytes 76808 | tf_op jit(solution)/shard_map/ppermute | solution.py:668
  32.1 35.5 %collective-permute-start.132 = (f32[5,8,128]{2,1,0:T(8,128)S(1)}, f32[5,8,128]{2,1,0:T(8,128)S(1)}, u32[]{:S(2)}, u32[]{:S(2)}) collective-permute-start(f32[5,8,128]{2,1,0:T(8,128)S(1)} %get-tuple-element.686), channel_id=1, source_target_pairs={{0,1},{1,0},{2,3},{3,2},{4,5},{5,4},{6,7},{7,6},{8,9},{9,8},{10,11... | collective-permute-start | bytes 61448 | tf_op jit(solution)/shard_map/ppermute | solution.py:668
  65.8 1.8 %collective-permute-start.133 = (f32[5,8,128]{2,1,0:T(8,128)S(1)}, f32[5,8,128]{2,1,0:T(8,128)S(1)}, u32[]{:S(2)}, u32[]{:S(2)}) collective-permute-start(f32[5,8,128]{2,1,0:T(8,128)S(1)} %get-tuple-element.687), channel_id=1, source_target_pairs={{0,4},{1,2},{2,1},{3,7},{4,0},{5,6},{6,5},{7,3},{8,12},{9,10},{10,... | collective-permute-start | bytes 61448 | tf_op jit(solution)/shard_map/ppermute | solution.py:679
  70.1 4.8 %collective-permute-start.134 = (f32[2,25,128]{2,1,0:T(8,128)S(1)}, f32[2,25,128]{2,1,0:T(8,128)S(1)}, u32[]{:S(2)}, u32[]{:S(2)}) collective-permute-start(f32[2,25,128]{2,1,0:T(8,128)S(1)} %get-tuple-element.690), channel_id=1, source_target_pairs={{0,4},{4,0},{8,12},{12,8},{16,20},{20,16},{24,28},{28,24},{1,5},{5... | collective-permute-start | bytes 76808 | tf_op jit(solution)/shard_map/ppermute | solution.py:668
  70.2 4.7 %collective-permute-start.135 = (f32[2,25,128]{2,1,0:T(8,128)S(1)}, f32[2,25,128]{2,1,0:T(8,128)S(1)}, u32[]{:S(2)}, u32[]{:S(2)}) collective-permute-start(f32[2,25,128]{2,1,0:T(8,128)S(1)} %get-tuple-element.691), channel_id=1, source_target_pairs={{0,28},{4,8},{8,4},{12,16},{16,12},{20,24},{24,20},{28,0},{1,29},{... | collective-permute-start | bytes 76808 | tf_op jit(solution)/shard_map/ppermute | solution.py:668
  70.9 3.9 %collective-permute-start.136 = (f32[5,8,128]{2,1,0:T(8,128)S(1)}, f32[5,8,128]{2,1,0:T(8,128)S(1)}, u32[]{:S(2)}, u32[]{:S(2)}) collective-permute-start(f32[5,8,128]{2,1,0:T(8,128)S(1)} %get-tuple-element.692), channel_id=1, source_target_pairs={{0,1},{1,0},{2,3},{3,2},{4,5},{5,4},{6,7},{7,6},{8,9},{9,8},{10,11... | collective-permute-start | bytes 61448 | tf_op jit(solution)/shard_map/ppermute | solution.py:668
  73.1 1.8 %collective-permute-start.137 = (f32[5,8,128]{2,1,0:T(8,128)S(1)}, f32[5,8,128]{2,1,0:T(8,128)S(1)}, u32[]{:S(2)}, u32[]{:S(2)}) collective-permute-start(f32[5,8,128]{2,1,0:T(8,128)S(1)} %get-tuple-element.693), channel_id=1, source_target_pairs={{0,4},{1,2},{2,1},{3,7},{4,0},{5,6},{6,5},{7,3},{8,12},{9,10},{10,... | collective-permute-start | bytes 61448 | tf_op jit(solution)/shard_map/ppermute | solution.py:679
  77.4 5.4 %collective-permute-start.138 = (f32[2,25,128]{2,1,0:T(8,128)S(1)}, f32[2,25,128]{2,1,0:T(8,128)S(1)}, u32[]{:S(2)}, u32[]{:S(2)}) collective-permute-start(f32[2,25,128]{2,1,0:T(8,128)S(1)} %get-tuple-element.696), channel_id=1, source_target_pairs={{0,4},{4,0},{8,12},{12,8},{16,20},{20,16},{24,28},{28,24},{1,5},{5... | collective-permute-start | bytes 76808 | tf_op jit(solution)/shard_map/ppermute | solution.py:668
  77.5 5.3 %collective-permute-start.139 = (f32[2,25,128]{2,1,0:T(8,128)S(1)}, f32[2,25,128]{2,1,0:T(8,128)S(1)}, u32[]{:S(2)}, u32[]{:S(2)}) collective-permute-start(f32[2,25,128]{2,1,0:T(8,128)S(1)} %get-tuple-element.697), channel_id=1, source_target_pairs={{0,28},{4,8},{8,4},{12,16},{16,12},{20,24},{24,20},{28,0},{1,29},{... | collective-permute-start | bytes 76808 | tf_op jit(solution)/shard_map/ppermute | solution.py:668
  79.0 3.8 %collective-permute-start.140 = (f32[5,8,128]{2,1,0:T(8,128)S(1)}, f32[5,8,128]{2,1,0:T(8,128)S(1)}, u32[]{:S(2)}, u32[]{:S(2)}) collective-permute-start(f32[5,8,128]{2,1,0:T(8,128)S(1)} %get-tuple-element.698), channel_id=1, source_target_pairs={{0,1},{1,0},{2,3},{3,2},{4,5},{5,4},{6,7},{7,6},{8,9},{9,8},{10,11... | collective-permute-start | bytes 61448 | tf_op jit(solution)/shard_map/ppermute | solution.py:668
  81.0 1.8 %collective-permute-start.141 = (f32[5,8,128]{2,1,0:T(8,128)S(1)}, f32[5,8,128]{2,1,0:T(8,128)S(1)}, u32[]{:S(2)}, u32[]{:S(2)}) collective-permute-start(f32[5,8,128]{2,1,0:T(8,128)S(1)} %get-tuple-element.699), channel_id=1, source_target_pairs={{0,4},{1,2},{2,1},{3,7},{4,0},{5,6},{6,5},{7,3},{8,12},{9,10},{10,... | collective-permute-start | bytes 61448 | tf_op jit(solution)/shard_map/ppermute | solution.py:679
  85.0 9.5 %copy-start.3 = (bf16[416,224]{1,0:T(8,128)(2,1)S(1)}, bf16[416,224]{1,0:T(8,128)(2,1)}, u32[]{:S(2)}) copy-start(bf16[416,224]{1,0:T(8,128)(2,1)} %get-tuple-element.670.proj_ref) | copy-start | bytes 559108
  85.1 6.8 %collective-permute-start.144 = (f32[3,8,128]{2,1,0:T(8,128)S(1)}, f32[3,8,128]{2,1,0:T(8,128)S(1)}, u32[]{:S(2)}, u32[]{:S(2)}) collective-permute-start(f32[3,8,128]{2,1,0:T(8,128)S(1)} %get-tuple-element.708), channel_id=1, source_target_pairs={{0,1},{1,0},{2,3},{3,2},{4,5},{5,4},{6,7},{7,6},{8,9},{9,8},{10,11... | collective-permute-start | bytes 36872 | tf_op jit(solution)/shard_map/ppermute | solution.py:668
  87.1 4.7 %collective-permute-start.145 = (f32[3,8,128]{2,1,0:T(8,128)S(1)}, f32[3,8,128]{2,1,0:T(8,128)S(1)}, u32[]{:S(2)}, u32[]{:S(2)}) collective-permute-start(f32[3,8,128]{2,1,0:T(8,128)S(1)} %get-tuple-element.709), channel_id=1, source_target_pairs={{0,4},{1,2},{2,1},{3,7},{4,0},{5,6},{6,5},{7,3},{8,12},{9,10},{10,... | collective-permute-start | bytes 36872 | tf_op jit(solution)/shard_map/ppermute | solution.py:679
  87.1 1.5 %collective-permute-start.142 = (f32[2,9,128]{2,1,0:T(8,128)S(1)}, f32[2,9,128]{2,1,0:T(8,128)S(1)}, u32[]{:S(2)}, u32[]{:S(2)}) collective-permute-start(f32[2,9,128]{2,1,0:T(8,128)S(1)} %get-tuple-element.706), channel_id=1, source_target_pairs={{0,4},{4,0},{8,12},{12,8},{16,20},{20,16},{24,28},{28,24},{1,5},{5... | collective-permute-start | bytes 27656 | tf_op jit(solution)/shard_map/ppermute | solution.py:668
  87.6 4.2 %collective-permute-start.143 = (f32[2,9,128]{2,1,0:T(8,128)S(1)}, f32[2,9,128]{2,1,0:T(8,128)S(1)}, u32[]{:S(2)}, u32[]{:S(2)}) collective-permute-start(f32[2,9,128]{2,1,0:T(8,128)S(1)} %get-tuple-element.707), channel_id=1, source_target_pairs={{0,28},{4,8},{8,4},{12,16},{16,12},{20,24},{24,20},{28,0},{1,29},{... | collective-permute-start | bytes 27656 | tf_op jit(solution)/shard_map/ppermute | solution.py:668
  93.0 4.8 %collective-permute-start.148 = (f32[3,8,128]{2,1,0:T(8,128)S(1)}, f32[3,8,128]{2,1,0:T(8,128)S(1)}, u32[]{:S(2)}, u32[]{:S(2)}) collective-permute-start(f32[3,8,128]{2,1,0:T(8,128)S(1)} %get-tuple-element.714), channel_id=1, source_target_pairs={{0,1},{1,0},{2,3},{3,2},{4,5},{5,4},{6,7},{7,6},{8,9},{9,8},{10,11... | collective-permute-start | bytes 36872 | tf_op jit(solution)/shard_map/ppermute | solution.py:668
  93.1 4.7 %collective-permute-start.149 = (f32[3,8,128]{2,1,0:T(8,128)S(1)}, f32[3,8,128]{2,1,0:T(8,128)S(1)}, u32[]{:S(2)}, u32[]{:S(2)}) collective-permute-start(f32[3,8,128]{2,1,0:T(8,128)S(1)} %get-tuple-element.715), channel_id=1, source_target_pairs={{0,4},{1,2},{2,1},{3,7},{4,0},{5,6},{6,5},{7,3},{8,12},{9,10},{10,... | collective-permute-start | bytes 36872 | tf_op jit(solution)/shard_map/ppermute | solution.py:679
  93.2 3.7 %collective-permute-start.146 = (f32[2,9,128]{2,1,0:T(8,128)S(1)}, f32[2,9,128]{2,1,0:T(8,128)S(1)}, u32[]{:S(2)}, u32[]{:S(2)}) collective-permute-start(f32[2,9,128]{2,1,0:T(8,128)S(1)} %get-tuple-element.712), channel_id=1, source_target_pairs={{0,4},{4,0},{8,12},{12,8},{16,20},{20,16},{24,28},{28,24},{1,5},{5... | collective-permute-start | bytes 27656 | tf_op jit(solution)/shard_map/ppermute | solution.py:668
  93.7 4.1 %collective-permute-start.147 = (f32[2,9,128]{2,1,0:T(8,128)S(1)}, f32[2,9,128]{2,1,0:T(8,128)S(1)}, u32[]{:S(2)}, u32[]{:S(2)}) collective-permute-start(f32[2,9,128]{2,1,0:T(8,128)S(1)} %get-tuple-element.713), channel_id=1, source_target_pairs={{0,28},{4,8},{8,4},{12,16},{16,12},{20,24},{24,20},{28,0},{1,29},{... | collective-permute-start | bytes 27656 | tf_op jit(solution)/shard_map/ppermute | solution.py:668
  96.9 4.8 %copy-start.1 = (f32[20,104,128]{2,1,0:T(8,128)S(1)}, f32[20,104,128]{2,1,0:T(8,128)}, u32[]{:S(2)}) copy-start(f32[20,104,128]{2,1,0:T(8,128)} %get-tuple-element.673.sw_ref) | copy-start | bytes 3194884
  99.1 6.0 %collective-permute-start.152 = (f32[3,8,128]{2,1,0:T(8,128)S(1)}, f32[3,8,128]{2,1,0:T(8,128)S(1)}, u32[]{:S(2)}, u32[]{:S(2)}) collective-permute-start(f32[3,8,128]{2,1,0:T(8,128)S(1)} %get-tuple-element.720), channel_id=1, source_target_pairs={{0,1},{1,0},{2,3},{3,2},{4,5},{5,4},{6,7},{7,6},{8,9},{9,8},{10,11... | collective-permute-start | bytes 36872 | tf_op jit(solution)/shard_map/ppermute | solution.py:668
  100.5 4.6 %collective-permute-start.153 = (f32[3,8,128]{2,1,0:T(8,128)S(1)}, f32[3,8,128]{2,1,0:T(8,128)S(1)}, u32[]{:S(2)}, u32[]{:S(2)}) collective-permute-start(f32[3,8,128]{2,1,0:T(8,128)S(1)} %get-tuple-element.721), channel_id=1, source_target_pairs={{0,4},{1,2},{2,1},{3,7},{4,0},{5,6},{6,5},{7,3},{8,12},{9,10},{10,... | collective-permute-start | bytes 36872 | tf_op jit(solution)/shard_map/ppermute | solution.py:679
  100.5 3.9 %collective-permute-start.150 = (f32[2,9,128]{2,1,0:T(8,128)S(1)}, f32[2,9,128]{2,1,0:T(8,128)S(1)}, u32[]{:S(2)}, u32[]{:S(2)}) collective-permute-start(f32[2,9,128]{2,1,0:T(8,128)S(1)} %get-tuple-element.718), channel_id=1, source_target_pairs={{0,4},{4,0},{8,12},{12,8},{16,20},{20,16},{24,28},{28,24},{1,5},{5... | collective-permute-start | bytes 27656 | tf_op jit(solution)/shard_map/ppermute | solution.py:668
  101.0 4.1 %collective-permute-start.151 = (f32[2,9,128]{2,1,0:T(8,128)S(1)}, f32[2,9,128]{2,1,0:T(8,128)S(1)}, u32[]{:S(2)}, u32[]{:S(2)}) collective-permute-start(f32[2,9,128]{2,1,0:T(8,128)S(1)} %get-tuple-element.719), channel_id=1, source_target_pairs={{0,28},{4,8},{8,4},{12,16},{16,12},{20,24},{24,20},{28,0},{1,29},{... | collective-permute-start | bytes 27656 | tf_op jit(solution)/shard_map/ppermute | solution.py:668
